TPU v7x, 256 devices: a whole 4x4x8 slice. The times are simulated.
256 devices in a mesh: phi: 32 (over z, x_hi, core), eta: 8 (over y, x_lo).
Axes of the slice: x: 4 (x_hi: 2, x_lo: 2; x = x_hi * 2 + x_lo), y: 4, z: 8, core: 2. Of those that a mesh axis runs over, the one named last changes fastest.
Arguments:
- features: bfloat16 [32, 512, 1024], P(None, 'phi', 'eta'), may hold values from -6 to 6
- cotangent: bfloat16 [32, 512, 1024], P(None, 'phi', 'eta'), may hold values from -6 to 6
- kernel_a: bfloat16 [27, 32, 32], replicated, may hold values from -0.21875 to 0.21875
- kernel_b: bfloat16 [27, 64, 32], replicated, may hold values from -0.21875 to 0.21875
- mixing: bfloat16 [32, 64], replicated, may hold values from -0.75 to 0.75
Outputs:
- output: bfloat16 [32, 512, 1024], P(None, 'phi', 'eta')
- grad_input: bfloat16 [32, 512, 1024], P(None, 'phi', 'eta')
- grad_kernel_a: float32 [27, 32, 32], replicated
- grad_kernel_b: float32 [27, 64, 32], replicated
- grad_mixing: float32 [32, 64], replicated
All inputs are finite; a program needn't handle non-finite values.
Results may differ from a plain program's by a relative error of at most 0.012.
Values may be sent and summed in bfloat16 or wider, within the bound.
A program may use at most 128 MiB of HBM per device.

v0:
```python
import math

import jax
import jax.numpy as jnp
from jax import lax
from jax.sharding import PartitionSpec as P

LAYERS = 32


def with_halo(block, sides, width, periodic):
    for axis, dim in sides:
        count = lax.axis_size(axis)
        forward = [(i, i + 1) for i in range(count - 1)]
        if periodic:
            forward.append((count - 1, 0))
        backward = [(target, source) for source, target in forward]
        low = lax.ppermute(
            lax.slice_in_dim(block, block.shape[dim] - width, None, axis=dim), axis, forward
        )
        high = lax.ppermute(lax.slice_in_dim(block, 0, width, axis=dim), axis, backward)
        block = jnp.concatenate([low, block, high], axis=dim)
    return block


def together(arrays, axis):
    line, at, done = (jnp.concatenate([a.reshape(-1) for a in arrays]), 0, [])
    so_far = lax.psum(line, axis)
    for a in arrays:
        done.append(so_far[at : at + a.size].reshape(a.shape))
        at += a.size
    return tuple(done)


def shifted(padded, offset, extent):
    step_phi = offset // 9
    step_eta = offset // 3 % 3
    step_layer = offset % 3
    window = padded[
        :,
        step_phi : step_phi + extent[0],
        step_eta : step_eta + extent[1],
        step_layer : step_layer + extent[2],
    ]
    return window.reshape(padded.shape[0], -1)


def convolve(padded, weight):
    extent = (padded.shape[1] - 2, padded.shape[2] - 2, padded.shape[3] - 2)
    summed = jnp.zeros((weight.shape[1], extent[0] * extent[1] * extent[2]), jnp.float32)
    for offset in range(27):
        summed = summed + jnp.dot(
            weight[offset], shifted(padded, offset, extent), preferred_element_type=jnp.float32
        )
    return summed.reshape((weight.shape[1],) + extent)


def kernel_grad(padded, upstream):
    extent = upstream.shape[1:]
    flat_up = upstream.reshape(upstream.shape[0], -1)
    kernel_terms = [
        lax.dot_general(
            flat_up,
            shifted(padded, offset, extent),
            (((1,), (1,)), ((), ())),
            preferred_element_type=jnp.float32,
        )
        for offset in range(27)
    ]
    return jnp.stack(kernel_terms)


def flipped(weight):
    return jnp.transpose(weight[::-1], (0, 2, 1))


def block_view(fine_grid):
    chans, rows_phi, rows_eta, layer_count = fine_grid.shape
    return fine_grid.astype(jnp.float32).reshape(
        chans, rows_phi // 2, 2, rows_eta // 2, 2, layer_count
    )


def widened(coarse):
    return jnp.repeat(jnp.repeat(coarse, 2, axis=1), 2, axis=2)


def silu_slope(linear):
    logistic = jax.nn.sigmoid(linear)
    return logistic * (1.0 + linear * (1.0 - logistic))


def mix_channels(mixing, gated):
    flat_gated = gated.reshape(gated.shape[0], -1)
    mixed = jnp.dot(mixing, flat_gated, preferred_element_type=jnp.float32)
    return mixed.reshape((mixing.shape[0],) + gated.shape[1:])


def unfold(field):
    return field.reshape(field.shape[0], field.shape[1], -1, LAYERS)


def refold(field):
    return field.reshape(field.shape[0], field.shape[1], -1)


def layer_pad(values):
    return jnp.pad(values, ((0, 0), (0, 0), (0, 0), (1, 1)))


def fine_pad(values):
    looped = with_halo(values, (("phi", 1),), 1, True)
    edged = with_halo(looped, (("eta", 2),), 1, False)
    return layer_pad(edged)


def coarse_pad(values):
    looped = with_halo(values, (("phi", 1),), 1, True)
    edged = with_halo(looped, (("eta", 2),), 1, False)
    return layer_pad(edged)


def coarse_level(padded_coarse, folded, kernel_b, mixing, padder):
    linear_b = convolve(padded_coarse, kernel_b)
    gated = jax.nn.silu(linear_b).astype(jnp.bfloat16)
    projected = mix_channels(mixing, gated).astype(jnp.bfloat16)
    flat_folded = folded.reshape(folded.shape[0], -1)
    mix_sum = lax.dot_general(
        flat_folded,
        gated.reshape(gated.shape[0], -1),
        (((1,), (1,)), ((), ())),
        preferred_element_type=jnp.float32,
    )
    grad_gated = lax.dot_general(
        mixing, flat_folded, (((0,), (0,)), ((), ())), preferred_element_type=jnp.float32
    ).reshape(linear_b.shape)
    grad_linear_b = (grad_gated * silu_slope(linear_b)).astype(jnp.bfloat16)
    kernel_b_sum = kernel_grad(padded_coarse, grad_linear_b)
    grad_coarse = convolve(padder(grad_linear_b), flipped(kernel_b)).astype(jnp.bfloat16)
    return (projected, grad_coarse, kernel_b_sum, mix_sum)


def shards(features, cotangent, kernel_a, kernel_b, mixing):
    features = unfold(features)
    cotangent = unfold(cotangent)
    folded = block_view(cotangent).sum(axis=(2, 4)).astype(jnp.bfloat16)
    padded_fine = fine_pad(features)
    linear_a = convolve(padded_fine, kernel_a)
    hidden = jax.nn.silu(linear_a).astype(jnp.bfloat16)
    coarse = block_view(hidden).mean(axis=(2, 4)).astype(jnp.bfloat16)
    projected, grad_coarse, kernel_b_sum, mix_sum = coarse_level(
        coarse_pad(coarse), folded, kernel_b, mixing, coarse_pad
    )
    output = (hidden.astype(jnp.float32) + widened(projected.astype(jnp.float32))).astype(
        jnp.bfloat16
    )
    grad_hidden = cotangent.astype(jnp.float32) + 0.25 * widened(grad_coarse.astype(jnp.float32))
    grad_linear_a = (grad_hidden * silu_slope(linear_a)).astype(jnp.bfloat16)
    kernel_a_sum = kernel_grad(padded_fine, grad_linear_a)
    grad_input = convolve(fine_pad(grad_linear_a), flipped(kernel_a)).astype(jnp.bfloat16)
    totals = together((kernel_a_sum, kernel_b_sum, mix_sum), ("phi", "eta"))
    cell_count = (
        features.shape[1]
        * features.shape[2]
        * features.shape[3]
        * lax.axis_size("phi")
        * lax.axis_size("eta")
    )
    factor = 1.0 / math.sqrt(cell_count)
    return (
        refold(output),
        refold(grad_input),
        totals[0] * factor,
        totals[1] * factor,
        totals[2] * factor,
    )


def solution(mesh):
    in_specs = (P(None, "phi", "eta"), P(None, "phi", "eta"), P(), P(), P())
    out_specs = (P(None, "phi", "eta"), P(None, "phi", "eta"), P(), P(), P())
    return jax.shard_map(shards, mesh=mesh, in_specs=in_specs, out_specs=out_specs, check_vma=False)
```

profile of v0, /device:TPU:1, one launch (start us, length us, event | category | flops | bytes accessed | tf_op | source)
XLA Modules:
  0.0 663.7 jit_solution(10130130058830055707)
XLA Ops:
  8.8 4.2 collective-permute-start
  18.7 2.9 collective-permute-start.2
  29.3 4.4 fusion.354
  36.0 4.1 pad_maximum_fusion.5
  94.4 2.6 copy.346
  174.8 6.1 collective-permute-start.4
  187.9 4.2 collective-permute-start.6
  287.3 3.8 collective-permute-start.8
  291.1 3.5 collective-permute-start.9
  305.8 2.8 reshape.559
  313.1 2.7 collective-permute-start.10
  317.2 4.0 collective-permute-done.11
  332.8 3.4 fusion.110
  338.8 3.4 fusion.107
  344.8 3.4 fusion.104
  350.8 3.4 fusion.101
  360.3 3.4 fusion.98
  366.3 3.4 fusion.95
  372.3 3.4 fusion.92
  378.3 3.4 fusion.89
  384.3 3.4 fusion.86
  388.9 2.7 collective-permute-start.12
  391.6 4.1 collective-permute-start.13
  398.8 4.5 collective-permute-start.14
  414.8 4.6 fusion.351
  442.9 2.3 reshape.596
  446.3 2.3 reshape.597
  449.7 2.4 reshape.598
  454.1 2.4 reshape.599
  457.6 2.3 reshape.600
  461.0 2.3 reshape.601
  499.7 151.4 %all-reduce.6.cloned.1.call-done = f32[84992]{0:T(1024)} async-done(((f32[84992]{0:T(1024)}), f32[84992]{0:T(1024)}) %all-reduce.6.cloned.1.call-update) | async-done | bytes 339984 | tf_op jit(solution)/shard_map/psum | solution.py:28
  (632 shorter events, 389.8 us)
Async XLA Ops:
  7.2 8.0 %copy-start = (bf16[32,64]{1,0:T(8,128)(2,1)S(1)}, bf16[32,64]{1,0:T(8,128)(2,1)}, u32[]{:S(2)}) copy-start(bf16[32,64]{1,0:T(8,128)(2,1)} %param.9) | copy-start | bytes 12292
  7.2 643.9 %all-reduce.6.cloned.1.call-start = ((), (), s32[]{:S(2)}) async-start(), calls=%async_computation | async-start | bytes 679936 | tf_op jit(solution)/shard_map/psum | solution.py:28
  8.4 6.5 copy-start.45
  8.4 6.5 copy-start.48
  8.8 7.9 %collective-permute-start = (bf16[32,1,4,32]{3,0,2,1:T(8,128)(2,1)S(1)}, bf16[32,1,4,32]{3,0,2,1:T(8,128)(2,1)S(1)}, u32[]{:S(2)}, u32[]{:S(2)}) collective-permute-start(bf16[32,1,4,32]{3,0,2,1:T(8,128)(2,1)S(1)} %get-tuple-element.89), channel_id=1, source_target_pairs={{0,8},{8,16},{16,24},{24,32},{32,40},{40,48},{48,56},{56,64},{64,7... | collective-permute-start | bytes 24584 | tf_op jit(solution)/shard_map/ppermute | solution.py:18
  13.0 4.8 collective-permute-start.1
  17.9 10.0 %copy-start.13 = (bf16[32,18,4,32]{3,0,2,1:T(8,128)(2,1)}, bf16[32,18,4,32]{3,0,2,1:T(8,128)(2,1)S(1)}, u32[]{:S(2)}) copy-start(bf16[32,18,4,32]{3,0,2,1:T(8,128)(2,1)S(1)} %constant_dynamic-update-slice_fusion) | copy-start | bytes 442372
  18.7 7.5 %collective-permute-start.2 = (bf16[32,18,1,32]{3,0,2,1:T(8,128)(2,1)}, bf16[32,18,1,32]{3,0,2,1:T(8,128)(2,1)}, u32[]{:S(2)}, u32[]{:S(2)}) collective-permute-start(bf16[32,18,1,32]{3,0,2,1:T(8,128)(2,1)} %get-tuple-element.80), channel_id=1, source_target_pairs={{0,1},{1,2},{2,3},{3,4},{4,5},{5,6},{6,7},{8,9},{9,10},{10,11},{11... | collective-permute-start | bytes 110600 | tf_op jit(solution)/shard_map/ppermute | solution.py:18
  21.6 6.3 collective-permute-start.3
  40.2 113.7 %copy-start.2 = (bf16[32,16,4,32]{3,0,2,1:T(8,128)(2,1)}, bf16[32,16,4,32]{3,0,2,1:T(8,128)(2,1)S(1)}, u32[]{:S(2)}) copy-start(bf16[32,16,4,32]{3,0,2,1:T(8,128)(2,1)S(1)} %get-tuple-element.67) | copy-start | bytes 393220
  171.0 16.0 %copy-start.10 = (f32[32,2048]{1,0:T(8,128)}, f32[32,2048]{1,0:T(8,128)S(1)}, u32[]{:S(2)}) copy-start(f32[32,2048]{1,0:T(8,128)S(1)} %fusion.23) | copy-start | bytes 786436
  172.9 8.0 %copy-start.42 = (bf16[27,64,32]{1,2,0:T(8,128)(2,1)S(1)}, bf16[27,64,32]{1,2,0:T(8,128)(2,1)}, u32[]{:S(2)}) copy-start(bf16[27,64,32]{1,2,0:T(8,128)(2,1)} %param.8) | copy-start | bytes 331780
  174.7 9.1 %copy-start.54 = (f32[64,512]{1,0:T(8,128)S(1)}, f32[64,512]{1,0:T(8,128)}, u32[]{:S(2)}) copy-start(f32[64,512]{1,0:T(8,128)} %convolution_bitcast_fusion.23) | copy-start | bytes 393220
  174.8 13.0 %collective-permute-start.4 = (bf16[32,1,2,32]{3,0,2,1:T(8,128)(2,1)S(1)}, bf16[32,1,2,32]{3,0,2,1:T(8,128)(2,1)S(1)}, u32[]{:S(2)}, u32[]{:S(2)}) collective-permute-start(bf16[32,1,2,32]{3,0,2,1:T(8,128)(2,1)S(1)} %get-tuple-element.154), channel_id=1, source_target_pairs={{0,8},{8,16},{16,24},{24,32},{32,40},{40,48},{48,56},{56,64},{64,7... | collective-permute-start | bytes 12296 | tf_op jit(solution)/shard_map/ppermute | solution.py:18
  180.9 6.9 %collective-permute-start.5 = (bf16[32,1,2,32]{3,0,2,1:T(8,128)(2,1)S(1)}, bf16[32,1,2,32]{3,0,2,1:T(8,128)(2,1)S(1)}, u32[]{:S(2)}, u32[]{:S(2)}) collective-permute-start(bf16[32,1,2,32]{3,0,2,1:T(8,128)(2,1)S(1)} %get-tuple-element.155), channel_id=1, source_target_pairs={{8,0},{16,8},{24,16},{32,24},{40,32},{48,40},{56,48},{64,56},{72,6... | collective-permute-start | bytes 12296 | tf_op jit(solution)/shard_map/ppermute | solution.py:21
  187.9 7.3 %collective-permute-start.6 = (bf16[32,10,1,32]{3,0,2,1:T(8,128)(2,1)S(1)}, bf16[32,10,1,32]{3,0,2,1:T(8,128)(2,1)S(1)}, u32[]{:S(2)}, u32[]{:S(2)}) collective-permute-start(bf16[32,10,1,32]{3,0,2,1:T(8,128)(2,1)S(1)} %get-tuple-element.146), channel_id=1, source_target_pairs={{0,1},{1,2},{2,3},{3,4},{4,5},{5,6},{6,7},{8,9},{9,10},{10,11},{11... | collective-permute-start | bytes 61448 | tf_op jit(solution)/shard_map/ppermute | solution.py:18
  192.1 5.2 collective-permute-start.7
  265.0 10.0 %copy-start.100 = (bf16[32,512]{1,0:T(8,128)(2,1)S(1)}, bf16[32,512]{1,0:T(8,128)(2,1)}, u32[]{:S(2)}) copy-start(bf16[32,512]{1,0:T(8,128)(2,1)} %reshape.533) | copy-start | bytes 98308
  269.5 8.6 %copy-start.99 = (bf16[32,512]{1,0:T(8,128)(2,1)S(1)}, bf16[32,512]{1,0:T(8,128)(2,1)}, u32[]{:S(2)}) copy-start(bf16[32,512]{1,0:T(8,128)(2,1)} %reshape.536) | copy-start | bytes 98308
  284.6 10.0 %copy-start.94 = (bf16[32,10,1,32]{3,0,2,1:T(8,128)(2,1)S(1)}, bf16[32,10,1,32]{3,0,2,1:T(8,128)(2,1)}, u32[]{:S(2)}) copy-start(bf16[32,10,1,32]{3,0,2,1:T(8,128)(2,1)} %copy-done.93) | copy-start | bytes 61444
  287.3 25.7 %collective-permute-start.8 = (bf16[64,1,2,32]{0,3,2,1:T(8,128)(2,1)}, bf16[64,1,2,32]{0,3,2,1:T(8,128)(2,1)S(1)}, u32[]{:S(2)}, u32[]{:S(2)}) collective-permute-start(bf16[64,1,2,32]{0,3,2,1:T(8,128)(2,1)} %get-tuple-element.150), channel_id=1, source_target_pairs={{0,8},{8,16},{16,24},{24,32},{32,40},{40,48},{48,56},{56,64},{64,7... | collective-permute-start | bytes 24584 | tf_op jit(solution)/shard_map/ppermute | solution.py:18
  291.1 21.9 %collective-permute-start.9 = (bf16[64,1,2,32]{0,3,2,1:T(8,128)(2,1)S(1)}, bf16[64,1,2,32]{0,3,2,1:T(8,128)(2,1)S(1)}, u32[]{:S(2)}, u32[]{:S(2)}) collective-permute-start(bf16[64,1,2,32]{0,3,2,1:T(8,128)(2,1)S(1)} %get-tuple-element.151), channel_id=1, source_target_pairs={{8,0},{16,8},{24,16},{32,24},{40,32},{48,40},{56,48},{64,56},{72,6... | collective-permute-start | bytes 24584 | tf_op jit(solution)/shard_map/ppermute | solution.py:21
  313.1 4.1 collective-permute-start.10
  315.8 5.5 collective-permute-start.11
  383.0 8.5 %copy-start.112 = (bf16[32,1,4,32]{3,1,2,0:T(2,128)(2,1)S(1)}, bf16[32,1,4,32]{3,1,2,0:T(2,128)(2,1)}, u32[]{:S(2)}) copy-start(bf16[32,1,4,32]{3,1,2,0:T(2,128)(2,1)} %get-tuple-element.85) | copy-start | bytes 24580
  383.0 12.7 %copy-start.44 = (f32[55296]{0:T(1024)S(1)}, f32[55296]{0:T(1024)}, u32[]{:S(2)}) copy-start(f32[55296]{0:T(1024)} %reshape.616) | copy-start | bytes 663556
  388.9 9.6 %collective-permute-start.12 = (bf16[32,1,4,32]{3,1,2,0:T(2,128)(2,1)S(1)}, bf16[32,1,4,32]{3,1,2,0:T(2,128)(2,1)S(1)}, u32[]{:S(2)}, u32[]{:S(2)}) collective-permute-start(bf16[32,1,4,32]{3,1,2,0:T(2,128)(2,1)S(1)} %copy-done.113), channel_id=1, source_target_pairs={{0,8},{8,16},{16,24},{24,32},{32,40},{40,48},{48,56},{56,64},{64,7... | collective-permute-start | bytes 24584 | tf_op jit(solution)/shard_map/ppermute | solution.py:18
  391.6 7.0 %collective-permute-start.13 = (bf16[32,1,4,32]{3,1,2,0:T(2,128)(2,1)S(1)}, bf16[32,1,4,32]{3,1,2,0:T(2,128)(2,1)S(1)}, u32[]{:S(2)}, u32[]{:S(2)}) collective-permute-start(bf16[32,1,4,32]{3,1,2,0:T(2,128)(2,1)S(1)} %copy-done.112), channel_id=1, source_target_pairs={{8,0},{16,8},{24,16},{32,24},{40,32},{48,40},{56,48},{64,56},{72,6... | collective-permute-start | bytes 24584 | tf_op jit(solution)/shard_map/ppermute | solution.py:21
  398.8 9.3 %collective-permute-start.14 = (bf16[32,18,1,32]{3,1,2,0:T(8,128)(2,1)S(1)}, bf16[32,18,1,32]{3,1,2,0:T(8,128)(2,1)S(1)}, u32[]{:S(2)}, u32[]{:S(2)}) collective-permute-start(bf16[32,18,1,32]{3,1,2,0:T(8,128)(2,1)S(1)} %get-tuple-element.75), channel_id=1, source_target_pairs={{0,1},{1,2},{2,3},{3,4},{4,5},{5,6},{6,7},{8,9},{9,10},{10,11},{11... | collective-permute-start | bytes 110600 | tf_op jit(solution)/shard_map/ppermute | solution.py:18
  403.3 6.5 collective-permute-start.15
  449.7 6.8 %copy-start.21 = (bf16[32,16,4,32]{3,1,2,0:T(8,128)(2,1)S(1)}, bf16[32,16,4,32]{3,1,2,0:T(8,128)(2,1)}, u32[]{:S(2)}) copy-start(bf16[32,16,4,32]{3,1,2,0:T(8,128)(2,1)} %get-tuple-element.34) | copy-start | bytes 393220
  474.8 6.6 copy-start.16
  (99 other events, 259.8 us)
Sparse Core Ops, SparseCore 0:
  398.6 252.4 all-reduce.5
where the time goes:
time: 675 us; the launch traced here: 664 us
  local copies, waits for them, and re-layouts  288 us (43%)
  waiting for transfers between devices  162 us (24%)
  matrix products  132 us (20%)
  starting transfers between devices  43.8 us (6%)
  other arithmetic  21.2 us (3%)
  between operations  16.5 us (2%)
    psum x1, waiting for transfers between devices, together(): so_far = lax.psum(line, axis)  151 us
    reshape x78, local copies, waits for them, and re-layouts, shifted(): return window.reshape(padded.shape[0], -1)  130 us
    slice x87, local copies, waits for them, and re-layouts, shifted(): padded[:, step_phi:step_phi + extent[0], step_eta:step_eta + extent[1], s...  120 us
    dot_general x108, matrix products, convolve(): jnp.dot(weight[offset], shifted(padded, offset, extent), preferred_elemen...  68.3 us
    dot_general x54, matrix products, kernel_grad(): lax.dot_general(flat_up, shifted(padded, offset, extent), (((1,), (1,)),...  61.9 us
    ppermute x8, starting transfers between devices, with_halo(): lax.ppermute(lax.slice_in_dim(block, block.shape[dim] - width, None, axis...  31 us
  transfers between devices with their start and end apart: 17, of which 7 were waited for; matrix products, arithmetic and copies ran while one was open for 19% of the time, Pallas kernels for 0%

commit v1 on v0

v1 whole, which is shorter than its diff:
```python
import functools
import math

import jax
import jax.numpy as jnp
from jax import lax
from jax.experimental import pallas as pl
from jax.experimental.pallas import tpu as pltpu
from jax.sharding import PartitionSpec as P

BF = jnp.bfloat16
F32 = jnp.float32
MESH = pl.DeviceIdType.MESH
DIRS = ((0, 1), (0, -1), (1, 0), (1, 1), (1, -1), (-1, 0), (-1, 1), (-1, -1))
A_TILES = 14
B_TILES = 28


def lane_of(shape):
    return lax.broadcasted_iota(jnp.int32, shape, len(shape) - 1)


def roll(x, shift):
    shift %= 128
    return x if shift == 0 else pltpu.roll(x, shift, x.ndim - 1)


def dot(a, b):
    return jnp.dot(a, b, preferred_element_type=F32)


def dot_nt(a, b):
    return lax.dot_general(a, b, (((1,), (1,)), ((), ())), preferred_element_type=F32)


def zero(x):
    return jnp.zeros((), x.dtype)


def side_by_side(rows):
    return jnp.concatenate(rows, axis=1)


def by_quarter(v0, v1, v2, v3):
    lane = lane_of(v0.shape)
    return jnp.where(
        lane < 64, jnp.where(lane < 32, v0, v1), jnp.where(lane < 96, v2, v3)
    )


def pack_column(x, size, start):
    return by_quarter(
        *[roll(x[size * g : size * (g + 1)], 32 * g - start) for g in range(4)]
    )


def unpack_column(packed, want):
    return [roll(packed, want - 32 * g) for g in range(4)]


def pack_pair(x, y):
    return jnp.where(lane_of(x.shape) < 64, roll(x, -32), roll(y, 32))


def widen_columns(x):
    lane = lane_of(x.shape)
    return jnp.where(lane < 32, roll(x, -32), jnp.where(lane < 96, x, roll(x, 32)))


def pool_columns(x):
    lane = lane_of(x.shape)
    both = x + jnp.where(lane < 64, roll(x, 32), roll(x, -32))
    return jnp.where((lane >= 32) & (lane < 96), both, zero(x))


def layer_shifts(x):
    layer = lane_of(x.shape) % 32
    return [
        jnp.where(layer < 31, roll(x, -1), zero(x)),
        x,
        jnp.where(layer > 0, roll(x, 1), zero(x)),
    ]


def conv_rows(src, count, weight, outs, sink):
    layer = lane_of((outs, 128)) % 32
    flat = 3 * src.shape[1]
    for r in range(0, count, 2):
        pair = [src[r + i : r + i + 3].reshape(flat, 128) for i in range(2)]
        z = dot(weight, side_by_side(pair))
        for i in range(2):
            zi = z[:, 128 * i : 128 * (i + 1)]
            low = jnp.where(layer > 0, roll(zi[:outs], 1), 0.0)
            high = jnp.where(layer < 31, roll(zi[2 * outs :], -1), 0.0)
            sink[r + i] = zi[outs : 2 * outs] + low + high


def sigmoid(v):
    return 1.0 / (1.0 + jnp.exp(-v))


def kernel(n_phi, n_eta, scale, *refs):
    (f_ref, ct_ref, ka_ref, kb_ref, mix_ref, out_ref, gi_ref, gka_ref, gkb_ref, gm_ref) = refs[:10]
    (
        x_s, colx_s, rcx, rrx,
        fold_s, colf_s, rcf, rrf,
        colc_s, rowc_s, rcc, rrc,
        g_s, colg_s, rcg, rrg,
        sfa, scb, sgb, sga, lin_a_s, lin_b_s, gc_s, gi_s,
        pa, ra1, xa2, ra2, xa3, resa,
        pb, rb1, xb2, rb2, xb3, resb,
        h_send, h_recv, a_send, a_recv, b_send, b_recv,
    ) = refs[10:]
    p = lax.axis_index("phi")
    e = lax.axis_index("eta")
    g1, g2 = 2 * n_eta, n_phi // 2
    hi_bit = lax.rem(p // 2, 2)
    me1 = hi_bit * n_eta + e
    me2 = (p // 4) * 2 + lax.rem(p, 2)

    def halo_device(d):
        return (lax.rem(p + d[0] + n_phi, n_phi), lax.rem(e + d[1] + n_eta, n_eta))

    def plane_device(i):
        q = lax.rem(me1 + i, g1)
        return ((p // 4) * 4 + (q // n_eta) * 2 + lax.rem(p, 2), lax.rem(q, n_eta))

    def line_device(i):
        r = lax.rem(me2 + i, g2)
        return ((r // 2) * 4 + hi_bit * 2 + lax.rem(r, 2), e)

    barrier = pltpu.get_barrier_semaphore()
    targets = [halo_device(d) for d in DIRS]
    targets += [plane_device(i) for i in range(1, g1)]
    targets += [line_device(i) for i in range(1, g2)]
    for target in targets:
        pl.semaphore_signal(barrier, inc=1, device_id=target, device_id_type=MESH)

    pending = []

    def send(src, dst, ssem, rsem, target):
        copy = pltpu.make_async_remote_copy(
            src_ref=src, dst_ref=dst, send_sem=ssem, recv_sem=rsem,
            device_id=target, device_id_type=MESH,
        )
        copy.start()
        pending.append(copy)
        return copy

    def halo_start(which, cols, rows, rc, rr):
        copies = []
        for k, d in enumerate(DIRS):
            if k < 2:
                src, dst = cols[k], rc.at[k]
            else:
                src, dst = rows[0 if d[0] > 0 else 1], rr.at[k - 2]
            copies.append(send(src, dst, h_send.at[which, k], h_recv.at[which, k], halo_device(d)))
        return copies

    def halo_wait(copies):
        for copy in copies:
            copy.wait_recv()

    has_left = e > 0
    has_right = e < n_eta - 1
    lo32 = jnp.where(has_left, 32, 0)
    lo64 = jnp.where(has_left, 64, 0)
    hi96 = jnp.where(has_right, 96, 128)
    hi64 = jnp.where(has_right, 64, 128)

    x = jnp.transpose(f_ref[...], (1, 0, 2))
    x_s[...] = x
    colx_s[0] = pack_column(x, 4, 96)
    colx_s[1] = pack_column(x, 4, 0)
    pl.semaphore_wait(barrier, len(targets))
    halo_x = halo_start(
        0, (colx_s.at[0], colx_s.at[1]), (x_s.at[15], x_s.at[0]), rcx, rrx
    )

    ct = jnp.transpose(ct_ref[...], (1, 0, 2)).astype(F32).reshape(8, 2, 32, 128)
    fold = pool_columns(ct[:, 0] + ct[:, 1]).astype(BF)
    fold_s[...] = fold
    colf_s[0] = pack_column(fold, 2, 64)
    colf_s[1] = pack_column(fold, 2, 32)
    halo_f = halo_start(
        1, (colf_s.at[0], colf_s.at[1]), (fold_s.at[7], fold_s.at[0]), rcf, rrf
    )

    def forward_weight(ref):
        return jnp.concatenate(
            [side_by_side([ref[3 * ab + c] for ab in range(9)]) for c in range(3)], axis=0
        )

    def backward_weight(ref):
        return jnp.concatenate(
            [side_by_side([ref[26 - 3 * ab - c] for c in range(3)]) for ab in range(9)], axis=0
        ).T

    wa_f, wb_f = forward_weight(ka_ref), forward_weight(kb_ref)
    wa_b, wb_b = backward_weight(ka_ref), backward_weight(kb_ref)
    mix = mix_ref[...]
    mix_t = mix.T

    def fine_windows(dst, middle, rc, rr):
        rows = jnp.concatenate([rr[0:1], middle, rr[3:4]], axis=0)
        left = jnp.concatenate(
            [roll(rr[1:2], 32)] + unpack_column(rc[0], 0) + [roll(rr[4:5], 32)], axis=0
        )
        right = jnp.concatenate(
            [roll(rr[2:3], 96)] + unpack_column(rc[1], 96) + [roll(rr[5:6], 96)], axis=0
        )
        lane = lane_of(rows.shape)
        dst[:, 0:32, :] = jnp.where(
            lane < lo32, left, jnp.where(lane < 32, zero(rows), roll(rows, 32))
        )
        dst[:, 32:64, :] = rows
        dst[:, 64:96, :] = jnp.where(
            lane >= hi96, right, jnp.where(lane >= 96, zero(rows), roll(rows, -32))
        )

    halo_wait(halo_x)
    fine_windows(sfa, x, rcx, rrx)
    conv_rows(sfa, 16, wa_f, 32, lin_a_s)
    lin_a = lin_a_s[...]
    hidden = (lin_a / (1.0 + jnp.exp(-lin_a))).astype(BF).astype(F32).reshape(8, 2, 32, 128)
    coarse = (0.25 * pool_columns(hidden[:, 0] + hidden[:, 1])).astype(BF)

    colc_s[...] = pack_pair(coarse[0:4], coarse[4:8])
    rowc_s[0:1] = pack_pair(coarse[6:7], coarse[7:8])
    rowc_s[1:2] = pack_pair(coarse[0:1], coarse[1:2])
    halo_c = halo_start(2, (colc_s, colc_s), (rowc_s.at[0], rowc_s.at[1]), rcc, rrc)

    halo_wait(halo_f)
    fold_rows = jnp.concatenate([rrf[0:1], fold, rrf[3:4]], axis=0)
    fold_left = jnp.concatenate(
        [roll(rrf[1:2], 64)] + unpack_column(rcf[0], 0) + [roll(rrf[4:5], 64)], axis=0
    )
    fold_right = jnp.concatenate(
        [roll(rrf[2:3], 64)] + unpack_column(rcf[1], 96) + [roll(rrf[5:6], 64)], axis=0
    )
    lane = lane_of(fold_rows.shape)
    fold_wide = jnp.where(
        (lane >= 32) & (lane < 96),
        fold_rows,
        jnp.where(
            lane < lo32, fold_left, jnp.where(lane >= hi96, fold_right, zero(fold_rows))
        ),
    )

    halo_wait(halo_c)
    rows = jnp.concatenate(
        [roll(rrc[0:1], 32), roll(rrc[0:1], -32), coarse, roll(rrc[3:4], 32), roll(rrc[3:4], -32)],
        axis=0,
    )
    left = jnp.concatenate(
        [rrc[1:2], roll(rrc[1:2], 64), rcc[0], roll(rcc[0], 64), rrc[4:5], roll(rrc[4:5], 64)],
        axis=0,
    )
    right = jnp.concatenate(
        [roll(rrc[2:3], 64), rrc[2:3], roll(rcc[1], 64), rcc[1], roll(rrc[5:6], 64), rrc[5:6]],
        axis=0,
    )
    lane = lane_of(rows.shape)
    left = jnp.where(lane < lo64, left, zero(left))
    right = jnp.where(lane >= hi64, right, zero(right))
    scb[:, 0:32, :] = jnp.where(lane < 64, left, roll(rows, 32))
    scb[:, 32:64, :] = jnp.where(
        lane < 32, roll(left, -32), jnp.where(lane < 96, rows, roll(right, 32))
    )
    scb[:, 64:96, :] = jnp.where(lane < 64, roll(rows, -32), right)

    conv_rows(scb, 10, wb_f, 64, lin_b_s)
    lin_b = lin_b_s[...]
    sig_b = sigmoid(lin_b)
    slope_b = sig_b * (1.0 + lin_b * (1.0 - sig_b))
    gated = (lin_b * sig_b)[1:9].astype(BF)
    grad_gated = dot(mix_t, side_by_side([fold_wide[r] for r in range(10)]))
    grad_b = jnp.concatenate(
        [(grad_gated[:, 128 * r : 128 * (r + 1)] * slope_b[r]).astype(BF)[None] for r in range(10)],
        axis=0,
    )
    sgb[:, 0:64, :] = roll(grad_b, 32)
    sgb[:, 64:128, :] = grad_b
    sgb[:, 128:192, :] = roll(grad_b, -32)

    own = grad_b[1:9]
    lane = lane_of(own.shape)
    own = jnp.where((lane >= 32) & (lane < 96), own, zero(own))
    shifts = layer_shifts(own)
    up = side_by_side([jnp.concatenate([s[r] for s in shifts], axis=0) for r in range(8)])
    seen = side_by_side([scb[r + 1 : r + 4].reshape(288, 128) for r in range(8)])
    sum_b = dot_nt(up, seen).astype(BF)
    sum_m = dot_nt(
        side_by_side([fold[r] for r in range(8)]), side_by_side([gated[r] for r in range(8)])
    ).astype(BF)
    n_a, n_b = pa.shape[1], pb.shape[1]

    def put(buf, tile, value):
        n = buf.shape[1]
        buf[tile // n, tile % n] = value

    for i in range(12):
        for l in range(2):
            put(pb, 2 * i + l, sum_b[16 * i : 16 * i + 16, 128 * l : 128 * l + 128])
    rest = side_by_side([sum_b[48 * g : 48 * g + 48, 256:288] for g in range(4)])
    for i in range(3):
        put(pb, 24 + i, rest[16 * i : 16 * i + 16])
    put(pb, 27, side_by_side([sum_m[0:16], sum_m[16:32]]))
    for t in range(B_TILES, g1 * n_b):
        put(pb, t, jnp.zeros((16, 128), BF))

    def spread(buf, dst, ssem, rsem):
        return [
            send(
                buf.at[lax.rem(me1 + i, g1)], dst.at[i - 1],
                ssem.at[0, i], rsem.at[0, i], plane_device(i),
            )
            for i in range(1, g1)
        ]

    spread_b = spread(pb, rb1, b_send, b_recv)

    conv_rows(sgb, 8, wb_b, 32, gc_s)
    grad_coarse = widen_columns(gc_s[...].astype(BF).astype(F32))
    grad_hidden = jnp.concatenate(
        [(ct[:, i] + 0.25 * grad_coarse)[:, None] for i in range(2)], axis=1
    ).reshape(16, 32, 128)
    sig_a = sigmoid(lin_a)
    grad_a = (grad_hidden * (sig_a * (1.0 + lin_a * (1.0 - sig_a)))).astype(BF)
    g_s[...] = grad_a
    colg_s[0] = pack_column(grad_a, 4, 96)
    colg_s[1] = pack_column(grad_a, 4, 0)
    halo_g = halo_start(
        3, (colg_s.at[0], colg_s.at[1]), (g_s.at[15], g_s.at[0]), rcg, rrg
    )

    shifts = layer_shifts(grad_a)
    up = side_by_side([jnp.concatenate([s[r] for s in shifts], axis=0) for r in range(16)])
    seen = side_by_side([sfa[r : r + 3].reshape(288, 128) for r in range(16)])
    sum_a = dot_nt(up, seen).astype(BF)
    for i in range(6):
        for l in range(2):
            put(pa, 2 * i + l, sum_a[16 * i : 16 * i + 16, 128 * l : 128 * l + 128])
    rest = side_by_side([sum_a[32 * g : 32 * g + 32, 256:288] for g in range(3)])
    rest = jnp.concatenate([rest, jnp.zeros((32, 32), BF)], axis=1)
    for i in range(2):
        put(pa, 12 + i, rest[16 * i : 16 * i + 16])
    for t in range(A_TILES, g1 * n_a):
        put(pa, t, jnp.zeros((16, 128), BF))
    spread_a = spread(pa, ra1, a_send, a_recv)

    projected = dot(mix, side_by_side([gated[r] for r in range(8)])).astype(BF).astype(F32)
    projected = jnp.concatenate(
        [projected[:, 128 * r : 128 * (r + 1)][None] for r in range(8)], axis=0
    )
    projected = widen_columns(projected)
    output = jnp.concatenate(
        [(hidden[:, i] + projected)[:, None] for i in range(2)], axis=1
    ).reshape(16, 32, 128)
    out_ref[...] = jnp.transpose(output.astype(BF), (1, 0, 2))

    def cross(copies, buf, arrived, mine, slots, ssem, rsem):
        for copy in copies:
            copy.wait_recv()
        total = buf[me1].astype(F32)
        for i in range(g1 - 1):
            total = total + arrived[i].astype(F32)
        total = total.astype(BF)
        mine[...] = total
        slots[me2] = total
        return [
            send(mine, slots.at[me2], ssem.at[1, i], rsem.at[1, i], line_device(i))
            for i in range(1, g2)
        ]

    def wait_slots(copies, src, slots, count, me, ssem, rsem, stage):
        for i in range(1, count):
            slot = lax.rem(me + count - i, count)
            pltpu.make_async_remote_copy(
                src_ref=src, dst_ref=slots.at[slot], send_sem=ssem.at[stage, i],
                recv_sem=rsem.at[stage, i], device_id=(p, e), device_id_type=MESH,
            ).wait_recv()

    def gather(copies, mine2, slots, mine, result, ssem, rsem):
        wait_slots(copies, mine2, slots, g2, me2, ssem, rsem, 1)
        total = slots[0].astype(F32)
        for i in range(1, g2):
            total = total + slots[i].astype(F32)
        total = total.astype(BF)
        mine[...] = total
        result[me1] = total
        return [
            send(mine, result.at[me1], ssem.at[2, i], rsem.at[2, i], plane_device(i))
            for i in range(1, g1)
        ]

    cross_b = cross(spread_b, pb, rb1, xb2, rb2, b_send, b_recv)
    cross_a = cross(spread_a, pa, ra1, xa2, ra2, a_send, a_recv)

    halo_wait(halo_g)
    fine_windows(sga, grad_a, rcg, rrg)
    conv_rows(sga, 16, wa_b, 32, gi_s)
    gi_ref[...] = jnp.transpose(gi_s[...].astype(BF), (1, 0, 2))

    gather_b = gather(cross_b, xb2, rb2, xb3, resb, b_send, b_recv)
    gather_a = gather(cross_a, xa2, ra2, xa3, resa, a_send, a_recv)

    wait_slots(gather_b, xb3, resb, g1, me1, b_send, b_recv, 2)

    def tile(buf, t):
        n = buf.shape[1]
        return buf[t // n, t % n].astype(F32) * scale

    for c in range(3):
        for l in range(2):
            block = jnp.concatenate([tile(resb, 2 * (4 * c + j) + l) for j in range(4)], axis=0)
            for q in range(4):
                gkb_ref[(4 * l + q) * 3 + c] = block[:, 32 * q : 32 * q + 32]
    rest = jnp.concatenate([tile(resb, 24 + i) for i in range(3)], axis=0)
    rest = jnp.concatenate([rest[:, 32 * g : 32 * g + 32] for g in range(4)], axis=0)
    for c in range(3):
        gkb_ref[24 + c] = rest[64 * c : 64 * c + 64]
    last = tile(resb, 27)
    gm_ref[0:16, :] = last[:, 0:64]
    gm_ref[16:32, :] = last[:, 64:128]

    wait_slots(gather_a, xa3, resa, g1, me1, a_send, a_recv, 2)
    for c in range(3):
        for l in range(2):
            block = jnp.concatenate([tile(resa, 2 * (2 * c + j) + l) for j in range(2)], axis=0)
            for q in range(4):
                gka_ref[(4 * l + q) * 3 + c] = block[:, 32 * q : 32 * q + 32]
    rest = jnp.concatenate([tile(resa, 12 + i) for i in range(2)], axis=0)
    for c in range(3):
        gka_ref[24 + c] = rest[:, 32 * c : 32 * c + 32]

    for copy in pending:
        copy.wait_send()


def shards(n_phi, n_eta, features, cotangent, kernel_a, kernel_b, mixing):
    g1, g2 = 2 * n_eta, n_phi // 2
    n_a, n_b = -(-A_TILES // g1), -(-B_TILES // g1)
    cells = features.shape[1] * features.shape[2] * n_phi * n_eta
    field = jax.ShapeDtypeStruct(features.shape, BF)

    def vm(*shape, dtype=BF):
        return pltpu.VMEM(shape, dtype)

    def sums(n):
        return [
            vm(g1, n, 16, 128), vm(g1 - 1, n, 16, 128), vm(n, 16, 128),
            vm(g2, n, 16, 128), vm(n, 16, 128), vm(g1, n, 16, 128),
        ]

    def halo(n):
        return [vm(2, n, 32, 128), vm(6, 32, 128)]

    dma = pltpu.SemaphoreType.DMA
    wide = max(g1, g2)
    scratch = [
        vm(16, 32, 128), vm(2, 4, 32, 128), *halo(4),
        vm(8, 32, 128), vm(2, 2, 32, 128), *halo(2),
        vm(4, 32, 128), vm(2, 32, 128), *halo(4),
        vm(16, 32, 128), vm(2, 4, 32, 128), *halo(4),
        vm(18, 96, 128), vm(12, 96, 128), vm(10, 192, 128), vm(18, 96, 128),
        vm(16, 32, 128, dtype=F32), vm(10, 64, 128, dtype=F32),
        vm(8, 32, 128, dtype=F32), vm(16, 32, 128, dtype=F32),
        *sums(n_a), *sums(n_b),
        dma((4, 8)), dma((4, 8)),
        dma((3, wide)), dma((3, wide)), dma((3, wide)), dma((3, wide)),
    ]
    vmem = pl.BlockSpec(memory_space=pltpu.VMEM)
    return pl.pallas_call(
        functools.partial(kernel, n_phi, n_eta, 1.0 / math.sqrt(cells)),
        out_shape=(
            field,
            field,
            jax.ShapeDtypeStruct(kernel_a.shape, F32),
            jax.ShapeDtypeStruct(kernel_b.shape, F32),
            jax.ShapeDtypeStruct(mixing.shape, F32),
        ),
        in_specs=[vmem] * 5,
        out_specs=(vmem,) * 5,
        scratch_shapes=scratch,
        compiler_params=pltpu.CompilerParams(collective_id=0, has_side_effects=True),
        name="block_step",
    )(features, cotangent, kernel_a, kernel_b, mixing)


def solution(mesh):
    specs = (P(None, "phi", "eta"), P(None, "phi", "eta"), P(), P(), P())
    body = functools.partial(shards, mesh.shape["phi"], mesh.shape["eta"])
    return jax.shard_map(body, mesh=mesh, in_specs=specs, out_specs=specs, check_vma=False)
```

time: 675 us -> 52.7 us (0.08); the launches traced: 664 us -> 52.5 us
  local copies, waits for them, and re-layouts: 288 us -> 6.85 us
  waiting for transfers between devices: 162 us -> 0 us
  matrix products: 132 us -> 0 us
  Pallas kernels: 0 us -> 45 us
  starting transfers between devices: 43.8 us -> 0 us
  other arithmetic: 21.2 us -> 0 us
  between operations: 16.5 us -> 0.66 us
    psum x1 -> x0, waiting for transfers between devices: 151 us -> none  [together(): so_far = lax.psum(line, axis)]
    reshape x86 -> x0, local copies, waits for them, and re-layouts: 141 us -> none  [the longest x78 130 us: shifted(): return window.reshape(padded.shape[0], -1)]
    dot_general x165 -> x0, matrix products: 132 us -> none  [the longest x108 68.3 us: convolve(): jnp.dot(weight[offset], shifted(padded, offset, extent), preferred_elemen...]
    slice x94 -> x0, local copies, waits for them, and re-layouts: 123 us -> none  [the longest x87 120 us: shifted(): padded[:, step_phi:step_phi + extent[0], step_eta:step_eta + extent[1], s...]
    pallas_call x0 -> x1, Pallas kernels: none -> 45 us  [shards(): pl.pallas_call(functools.partial(kernel, n_phi, n_eta, 1.0 / math.sqrt(ce...]
    ppermute x16 -> x0, starting transfers between devices: 43.8 us -> none  [the longest x8 31 us: with_halo(): lax.ppermute(lax.slice_in_dim(block, block.shape[dim] - width, None, axis...]
    concatenate x14 -> x0, other arithmetic: 10.7 us -> none  [the longest x13 9.94 us: with_halo(): block = jnp.concatenate([low, block, high], axis=dim)]
    ppermute x16 -> x0, waiting for transfers between devices: 10.4 us -> none  [the longest x8 10.3 us: with_halo(): lax.ppermute(lax.slice_in_dim(block, 0, width, axis=dim), axis, backward)]
  transfers between devices with their start and end apart: 17 -> 0, of which waited for: 7 -> 0; matrix products, arithmetic and copies ran while one was open for 19% -> 0% of each run, Pallas kernels for 0% -> 0%
where the time goes in v1:
time: 52.7 us; the launch traced here: 52.5 us
  Pallas kernels  45 us (85%)
  local copies, waits for them, and re-layouts  6.85 us (13%)
  between operations  0.66 us (1%)
    pallas_call x1, Pallas kernels, shards(): pl.pallas_call(functools.partial(kernel, n_phi, n_eta, 1.0 / math.sqrt(ce...  45 us
    unnamed x13, local copies, waits for them, and re-layouts  4.59 us
    pallas_call x1, local copies, waits for them, and re-layouts, shards(): pl.pallas_call(functools.partial(kernel, n_phi, n_eta, 1.0 / math.sqrt(ce...  2.26 us

profile of v1, /device:TPU:1, one launch (start us, length us, event | category | flops | bytes accessed | tf_op | source)
XLA Modules:
  0.0 52.5 jit_solution(14312100727541897717)
XLA Ops:
  0.6 1.9 %copy.10.refs_3_ = bf16[27,64,32]{2,1,0:T(8,128)(2,1)} copy(bf16[27,64,32]{1,2,0:T(8,128)(2,1)} %param.8) | data formatting | bytes 221184 | tf_op args[3]
  2.5 45.0 %block_step.1 = (bf16[32,16,128]{2,1,0:T(8,128)(2,1)}, bf16[32,16,128]{2,1,0:T(8,128)(2,1)}, f32[27,32,32]{2,1,0:T(8,128)}, f32[27,64,32]{2,1,0:T(8,128)}, f32[32,64]{1,0:T(8,128)}) custom-call(bf16[32,16,128]{2,1,0:T(8,128)(2,1)} %refs_0_.1, bf16[32,16,128]{2,1,0:T(8,128)(2,1)} %refs_1_.1, bf16[27,32,32]{2,1,0:T(8,128)(2,1)} %refs_2_.1, ...), custom_call_target="tpu_custom_call" | custom-call | tf_op jit(solution)/shard_map/block_step/pallas_call | solution.py:474
  47.6 0.0 copy-start.2
  47.6 0.0 copy-start.1
  47.6 2.3 %copy.11 = f32[27,64,32]{1,2,0:T(8,128)} copy(f32[27,64,32]{2,1,0:T(8,128)} %get-tuple-element.8) | data formatting | bytes 442368 | tf_op jit(solution)/shard_map/block_step/pallas_call | solution.py:474
  49.8 0.0 copy-done.2
  49.8 0.0 copy-start
  49.8 0.7 %copy.16 = bf16[32,16,128]{2,1,0:T(8,128)(2,1)} copy(bf16[32,16,128]{2,1,0:T(8,128)(2,1)S(1)} %copy-done.2) | data formatting | bytes 262144
  50.5 0.0 copy-done.1
  50.5 0.7 %copy.17 = bf16[32,16,128]{2,1,0:T(8,128)(2,1)} copy(bf16[32,16,128]{2,1,0:T(8,128)(2,1)S(1)} %copy-done.1) | data formatting | bytes 262144
  51.2 0.0 copy-done
  51.2 0.0 copy-start.3
  51.2 0.8 %copy.18 = f32[27,32,32]{2,1,0:T(8,128)} copy(f32[27,32,32]{2,1,0:T(8,128)S(1)} %copy-done) | data formatting | bytes 221184
  51.9 0.0 copy-done.3
  51.9 0.6 %copy.19 = f32[32,64]{1,0:T(8,128)} copy(f32[32,64]{1,0:T(8,128)S(1)} %copy-done.3) | data formatting | bytes 16384
Async XLA Ops:
  47.6 2.3 %copy-start.2 = (bf16[32,16,128]{2,1,0:T(8,128)(2,1)S(1)}, bf16[32,16,128]{2,1,0:T(8,128)(2,1)}, u32[]{:S(2)}) copy-start(bf16[32,16,128]{2,1,0:T(8,128)(2,1)} %get-tuple-element.15) | copy-start | bytes 393220
  47.6 2.9 %copy-start.1 = (bf16[32,16,128]{2,1,0:T(8,128)(2,1)S(1)}, bf16[32,16,128]{2,1,0:T(8,128)(2,1)}, u32[]{:S(2)}) copy-start(bf16[32,16,128]{2,1,0:T(8,128)(2,1)} %get-tuple-element.16) | copy-start | bytes 393220
  49.8 1.3 %copy-start = (f32[27,32,32]{2,1,0:T(8,128)S(1)}, f32[27,32,32]{2,1,0:T(8,128)}, u32[]{:S(2)}) copy-start(f32[27,32,32]{2,1,0:T(8,128)} %get-tuple-element.17) | copy-start | bytes 331780
  51.2 0.8 %copy-start.3 = (f32[32,64]{1,0:T(8,128)S(1)}, f32[32,64]{1,0:T(8,128)}, u32[]{:S(2)}) copy-start(f32[32,64]{1,0:T(8,128)} %get-tuple-element.19) | copy-start | bytes 24580

commit v2 on v1

v2 whole, which is shorter than its diff:
```python
import functools
import math

import jax
import jax.numpy as jnp
from jax import lax
from jax.experimental import pallas as pl
from jax.experimental.pallas import tpu as pltpu
from jax.sharding import PartitionSpec as P

BF = jnp.bfloat16
F32 = jnp.float32
MESH = pl.DeviceIdType.MESH
DIRS = ((0, 1), (0, -1), (1, 0), (1, 1), (1, -1), (-1, 0), (-1, 1), (-1, -1))
PLANE = 32


def lane_of(shape):
    return lax.broadcasted_iota(jnp.int32, shape, len(shape) - 1)


def roll(x, shift):
    shift %= 128
    return x if shift == 0 else pltpu.roll(x, shift, x.ndim - 1)


def dot(a, b):
    return jnp.dot(a, b, preferred_element_type=F32)


def dot_nt(a, b):
    return lax.dot_general(a, b, (((1,), (1,)), ((), ())), preferred_element_type=F32)


def zero(x):
    return jnp.zeros((), x.dtype)


def side_by_side(rows):
    return jnp.concatenate(rows, axis=1)


def by_quarter(v0, v1, v2, v3):
    lane = lane_of(v0.shape)
    return jnp.where(
        lane < 64, jnp.where(lane < 32, v0, v1), jnp.where(lane < 96, v2, v3)
    )


def pack_column(x, size, start):
    return by_quarter(
        *[roll(x[size * g : size * (g + 1)], 32 * g - start) for g in range(4)]
    )


def unpack_column(packed, want):
    return [roll(packed, want - 32 * g) for g in range(4)]


def pack_pair(x, y):
    return jnp.where(lane_of(x.shape) < 64, roll(x, -32), roll(y, 32))


def widen_columns(x):
    lane = lane_of(x.shape)
    return jnp.where(lane < 32, roll(x, -32), jnp.where(lane < 96, x, roll(x, 32)))


def pool_columns(x):
    lane = lane_of(x.shape)
    both = x + jnp.where(lane < 64, roll(x, 32), roll(x, -32))
    return jnp.where((lane >= 32) & (lane < 96), both, zero(x))


def layer_shifts(x):
    layer = lane_of(x.shape) % 32
    return [
        jnp.where(layer < 31, roll(x, -1), zero(x)),
        x,
        jnp.where(layer > 0, roll(x, 1), zero(x)),
    ]


def conv_rows(src, count, weight, outs, sink):
    layer = lane_of((outs, 128)) % 32
    flat = 3 * src.shape[1]
    for r in range(0, count, 2):
        pair = [src[r + i : r + i + 3].reshape(flat, 128) for i in range(2)]
        z = dot(weight, side_by_side(pair))
        for i in range(2):
            zi = z[:, 128 * i : 128 * (i + 1)]
            low = jnp.where(layer > 0, roll(zi[:outs], 1), 0.0)
            high = jnp.where(layer < 31, roll(zi[2 * outs :], -1), 0.0)
            sink[r + i] = zi[outs : 2 * outs] + low + high


def sigmoid(v):
    return 1.0 / (1.0 + jnp.exp(-v))


def kernel(n_phi, n_eta, scale, *refs):
    ins, (out_ref, gi_ref, gka_ref, gkb_ref, gm_ref) = refs[:5], refs[5:10]
    (
        f_ref, ct_ref, ka_ref, kb_ref, mix_ref, load_sem,
        x_s, colx_s, rx,
        fold_s, colf_s, rf,
        colc_s, rowc_s, rc,
        g_s, colg_s, rg,
        sfa, scb, sgb, sga, slope_a_s, lin_a_s, lin_b_s, gc_s, gi_s,
        pa, ra, pb, rb, x2, r2, x3, res,
        h_send, h_recv, s_send, s_recv,
    ) = refs[10:]
    p = lax.axis_index("phi")
    e = lax.axis_index("eta")
    g1, g2 = 4 * n_eta, n_phi // 4
    me1 = lax.rem(p, 4) * n_eta + e
    me2 = p // 4

    def wrap(i, n):
        return jnp.where(i >= n, i - n, i)

    def halo_device(d):
        return (wrap(p + d[0] % n_phi, n_phi), wrap(e + d[1] % n_eta, n_eta))

    def plane_device(i):
        q = wrap(me1 + i, g1)
        return (me2 * 4 + q // n_eta, lax.rem(q, n_eta))

    def line_device(i):
        r = wrap(me2 + i, g2)
        return (r * 4 + lax.rem(p, 4), e)

    barrier = pltpu.get_barrier_semaphore()
    targets = [line_device(i) for i in sorted(range(1, g2), key=lambda i: -min(i, g2 - i))]
    targets += [plane_device(i) for i in range(1, g1)]
    targets += [halo_device(d) for d in DIRS]
    for target in targets:
        pl.semaphore_signal(barrier, inc=1, device_id=target, device_id_type=MESH)

    loads = [
        pltpu.make_async_copy(src, dst, load_sem.at[k])
        for k, (src, dst) in enumerate(zip(ins, (f_ref, ct_ref, ka_ref, kb_ref, mix_ref)))
    ]
    for load in loads:
        load.start()

    departures = []

    def send(src, dst, ssem, rsem, target):
        pltpu.make_async_remote_copy(
            src_ref=src, dst_ref=dst, send_sem=ssem, recv_sem=rsem,
            device_id=target, device_id_type=MESH,
        ).start()

    def whole(ref, ssem, rsem):
        return pltpu.make_async_remote_copy(
            src_ref=ref, dst_ref=ref, send_sem=ssem, recv_sem=rsem,
            device_id=(p, e), device_id_type=MESH,
        )

    def halo_start(which, cols, rows, arrived):
        n = (arrived.shape[0] - 6) // 2
        ssem, rsem = h_send.at[which], h_recv.at[which]
        for k, d in enumerate(DIRS):
            if k < 2:
                src, dst = cols[k], arrived.at[pl.ds(n * k, n)]
            else:
                src, dst = rows[0 if d[0] > 0 else 1], arrived.at[2 * n + k - 2]
            send(src, dst, ssem, rsem, halo_device(d))
        copy = whole(arrived, ssem, rsem)
        departures.append(copy)
        return copy

    def halo_parts(arrived):
        n = (arrived.shape[0] - 6) // 2
        rows = [arrived[2 * n + j : 2 * n + j + 1] for j in range(6)]
        return (arrived[0:n], arrived[n : 2 * n]), rows

    has_left = e > 0
    has_right = e < n_eta - 1
    lo32 = jnp.where(has_left, 32, 0)
    lo64 = jnp.where(has_left, 64, 0)
    hi96 = jnp.where(has_right, 96, 128)
    hi64 = jnp.where(has_right, 64, 128)

    loads[0].wait()
    x = jnp.transpose(f_ref[...], (1, 0, 2))
    x_s[...] = x
    colx_s[0] = pack_column(x, 4, 96)
    colx_s[1] = pack_column(x, 4, 0)
    pl.semaphore_wait(barrier, len(targets))
    halo_x = halo_start(
        0, (colx_s.at[0], colx_s.at[1]), (x_s.at[15], x_s.at[0]), rx
    )

    for load in loads[1:]:
        load.wait()
    ct = jnp.transpose(ct_ref[...], (1, 0, 2)).astype(F32).reshape(8, 2, 32, 128)
    fold = pool_columns(ct[:, 0] + ct[:, 1]).astype(BF)
    fold_s[...] = fold
    colf_s[0] = pack_column(fold, 2, 64)
    colf_s[1] = pack_column(fold, 2, 32)
    halo_f = halo_start(
        1, (colf_s.at[0], colf_s.at[1]), (fold_s.at[7], fold_s.at[0]), rf
    )

    def forward_weight(ref):
        return jnp.concatenate(
            [side_by_side([ref[3 * ab + c] for ab in range(9)]) for c in range(3)], axis=0
        )

    def backward_weight(ref):
        return jnp.concatenate(
            [side_by_side([ref[26 - 3 * ab - c] for c in range(3)]) for ab in range(9)], axis=0
        ).T

    wa_f, wa_b = forward_weight(ka_ref), backward_weight(ka_ref)
    wb_f = jnp.concatenate(
        [side_by_side([kb_ref[3 * ab + c] for c in range(3)]) for ab in range(9)], axis=0
    ).T
    wb_b = jnp.concatenate(
        [side_by_side([kb_ref[26 - 3 * ab - c] for ab in range(9)]) for c in range(3)], axis=0
    )
    mix = mix_ref[...]
    mix_t = mix.T

    def fine_windows(dst, middle, arrived):
        cols, rim = halo_parts(arrived)
        rows = jnp.concatenate([rim[0], middle, rim[3]], axis=0)
        left = jnp.concatenate(
            [roll(rim[1], 32)] + unpack_column(cols[0], 0) + [roll(rim[4], 32)], axis=0
        )
        right = jnp.concatenate(
            [roll(rim[2], 96)] + unpack_column(cols[1], 96) + [roll(rim[5], 96)], axis=0
        )
        lane = lane_of(rows.shape)
        dst[:, 0:32, :] = jnp.where(
            lane < lo32, left, jnp.where(lane < 32, zero(rows), roll(rows, 32))
        )
        dst[:, 32:64, :] = rows
        dst[:, 64:96, :] = jnp.where(
            lane >= hi96, right, jnp.where(lane >= 96, zero(rows), roll(rows, -32))
        )

    halo_x.wait_recv()
    fine_windows(sfa, x, rx)
    conv_rows(sfa, 16, wa_f, 32, lin_a_s)
    lin_a = lin_a_s[...]
    hidden = (lin_a / (1.0 + jnp.exp(-lin_a))).astype(BF).astype(F32).reshape(8, 2, 32, 128)
    coarse = (0.25 * pool_columns(hidden[:, 0] + hidden[:, 1])).astype(BF)

    colc_s[...] = pack_pair(coarse[0:4], coarse[4:8])
    rowc_s[0:1] = pack_pair(coarse[6:7], coarse[7:8])
    rowc_s[1:2] = pack_pair(coarse[0:1], coarse[1:2])
    halo_c = halo_start(2, (colc_s, colc_s), (rowc_s.at[0], rowc_s.at[1]), rc)

    halo_f.wait_recv()
    cols, rim = halo_parts(rf)
    fold_rows = jnp.concatenate([rim[0], fold, rim[3]], axis=0)
    fold_left = jnp.concatenate(
        [roll(rim[1], 64)] + unpack_column(cols[0], 0) + [roll(rim[4], 64)], axis=0
    )
    fold_right = jnp.concatenate(
        [roll(rim[2], 64)] + unpack_column(cols[1], 96) + [roll(rim[5], 64)], axis=0
    )
    lane = lane_of(fold_rows.shape)
    fold_wide = jnp.where(
        (lane >= 32) & (lane < 96),
        fold_rows,
        jnp.where(
            lane < lo32, fold_left, jnp.where(lane >= hi96, fold_right, zero(fold_rows))
        ),
    )

    grad_gated = dot(mix_t, side_by_side([fold_wide[r] for r in range(10)]))
    sig_a = sigmoid(lin_a)
    slope_a_s[...] = sig_a * (1.0 + lin_a * (1.0 - sig_a))

    halo_c.wait_recv()
    cols, rim = halo_parts(rc)
    rows = jnp.concatenate(
        [roll(rim[0], 32), roll(rim[0], -32), coarse, roll(rim[3], 32), roll(rim[3], -32)],
        axis=0,
    )
    left = jnp.concatenate(
        [rim[1], roll(rim[1], 64), cols[0], roll(cols[0], 64), rim[4], roll(rim[4], 64)],
        axis=0,
    )
    right = jnp.concatenate(
        [roll(rim[2], 64), rim[2], roll(cols[1], 64), cols[1], roll(rim[5], 64), rim[5]],
        axis=0,
    )
    lane = lane_of(rows.shape)
    left = jnp.where(lane < lo64, left, zero(left))
    right = jnp.where(lane >= hi64, right, zero(right))
    scb[:, 0:32, :] = jnp.where(lane < 64, left, roll(rows, 32))
    scb[:, 32:64, :] = jnp.where(
        lane < 32, roll(left, -32), jnp.where(lane < 96, rows, roll(right, 32))
    )
    scb[:, 64:96, :] = jnp.where(lane < 64, roll(rows, -32), right)

    conv_rows(scb, 10, wb_f, 64, lin_b_s)
    lin_b = lin_b_s[...]
    sig_b = sigmoid(lin_b)
    slope_b = sig_b * (1.0 + lin_b * (1.0 - sig_b))
    gated = (lin_b * sig_b)[1:9].astype(BF)
    grad_b = jnp.concatenate(
        [(grad_gated[:, 128 * r : 128 * (r + 1)] * slope_b[r]).astype(BF)[None] for r in range(10)],
        axis=0,
    )
    sgb[:, 0:64, :] = roll(grad_b, 32)
    sgb[:, 64:128, :] = grad_b
    sgb[:, 128:192, :] = roll(grad_b, -32)

    own = grad_b[1:9]
    lane = lane_of(own.shape)
    own = jnp.where((lane >= 32) & (lane < 96), own, zero(own))
    shifts = layer_shifts(own)
    up = side_by_side([jnp.concatenate([s[r] for s in shifts], axis=0) for r in range(8)])
    seen = side_by_side([scb[r + 1 : r + 4].reshape(288, 128) for r in range(8)])
    sum_b = dot_nt(seen, up)
    sum_m = dot_nt(
        side_by_side([fold[r] for r in range(8)]), side_by_side([gated[r] for r in range(8)])
    )
    for i in range(18):
        pb[i] = sum_b[16 * i : 16 * i + 16, 0:128].astype(BF)
    rest = side_by_side([sum_b[144 * g : 144 * g + 144, 128:192] for g in range(2)])
    for i in range(9):
        pb[18 + i] = rest[16 * i : 16 * i + 16].astype(BF)
    pb[27] = side_by_side([sum_m[0:16], sum_m[16:32]]).astype(BF)
    for t in range(28, PLANE):
        pb[t] = jnp.zeros((16, 128), BF)

    def spread(buf, dst, k):
        for i in range(1, g1):
            q = wrap(me1 + i, g1)
            send(buf.at[q], dst.at[i - 1], s_send.at[k], s_recv.at[k], plane_device(i))
        copy = whole(dst, s_send.at[k], s_recv.at[k])
        departures.append(copy)
        return copy

    spread_b = spread(pb, rb, 0)

    conv_rows(sgb, 8, wb_b, 32, gc_s)
    grad_coarse = widen_columns(gc_s[...].astype(BF).astype(F32))
    grad_hidden = jnp.concatenate(
        [(ct[:, i] + 0.25 * grad_coarse)[:, None] for i in range(2)], axis=1
    ).reshape(16, 32, 128)
    grad_a = (grad_hidden * slope_a_s[...]).astype(BF)
    g_s[...] = grad_a
    colg_s[0] = pack_column(grad_a, 4, 96)
    colg_s[1] = pack_column(grad_a, 4, 0)
    shifts = layer_shifts(grad_a)
    up = side_by_side([jnp.concatenate([s[r] for s in shifts], axis=0) for r in range(16)])
    seen = side_by_side([sfa[r : r + 3].reshape(288, 128) for r in range(16)])
    sum_a = dot_nt(up, seen)
    for i in range(12):
        for l in range(2):
            pa[2 * i + l] = sum_a[8 * i : 8 * i + 8, 128 * l : 128 * l + 128].astype(BF)
    rest = side_by_side([sum_a[32 * g : 32 * g + 32, 256:288] for g in range(3)])
    rest = jnp.concatenate([rest, jnp.zeros((32, 32), F32)], axis=1)
    for i in range(4):
        pa[24 + i] = rest[8 * i : 8 * i + 8].astype(BF)
    for t in range(28, PLANE):
        pa[t] = jnp.zeros((8, 128), BF)
    spread_a = spread(pa, ra, 1)
    projected = dot(mix, side_by_side([gated[r] for r in range(8)])).astype(BF).astype(F32)
    projected = jnp.concatenate(
        [projected[:, 128 * r : 128 * (r + 1)][None] for r in range(8)], axis=0
    )
    projected = widen_columns(projected)
    output = jnp.concatenate(
        [(hidden[:, i] + projected)[:, None] for i in range(2)], axis=1
    ).reshape(16, 32, 128)
    out_ref[...] = jnp.transpose(output.astype(BF), (1, 0, 2))

    spread_b.wait_recv()
    total_b = pb[me1].astype(F32)
    for i in range(g1 - 1):
        total_b = total_b + rb[i].astype(F32)
    spread_a.wait_recv()
    total_a = pa[me1].astype(F32)
    for i in range(g1 - 1):
        total_a = total_a + ra[i].astype(F32)
    total = jnp.concatenate([total_b, total_a], axis=0).astype(BF)
    x2[...] = total
    r2[me2] = total
    for i in range(1, g2):
        send(x2, r2.at[me2], s_send.at[2], s_recv.at[2], line_device(i))
    crossed = whole(r2.at[pl.ds(0, g2 - 1)], s_send.at[2], s_recv.at[2])
    departures.append(crossed)

    halo_g = halo_start(
        3, (colg_s.at[0], colg_s.at[1]), (g_s.at[15], g_s.at[0]), rg
    )

    crossed.wait_recv()
    total = r2[0].astype(F32)
    for i in range(1, g2):
        total = total + r2[i].astype(F32)
    total = total.astype(BF)
    x3[...] = total
    res[me1] = total
    for i in range(1, g1):
        send(x3, res.at[me1], s_send.at[3], s_recv.at[3], plane_device(i))
    gathered = whole(res.at[pl.ds(0, g1 - 1)], s_send.at[3], s_recv.at[3])
    departures.append(gathered)
    halo_g.wait_recv()
    fine_windows(sga, grad_a, rg)
    conv_rows(sga, 16, wa_b, 32, gi_s)
    gi_ref[...] = jnp.transpose(gi_s[...].astype(BF), (1, 0, 2))

    gathered.wait_recv()

    for ab in range(9):
        for h in range(2):
            rows = slice(16 * h, 16 * h + 16)
            u = 2 * ab + h
            pair = res[u, 0:16].astype(F32) * scale
            gkb_ref[3 * ab, rows, :] = pair[:, 0:64]
            gkb_ref[3 * ab + 1, rows, :] = pair[:, 64:128]
            g = u // 9
            rest = res[18 + u % 9, 0:16].astype(F32) * scale
            gkb_ref[3 * ab + 2, rows, :] = rest[:, 64 * g : 64 * g + 64]
    last = res[27, 0:16].astype(F32) * scale
    gm_ref[0:16, :] = last[:, 0:64]
    gm_ref[16:32, :] = last[:, 64:128]

    for c in range(3):
        for h in range(4):
            rows = slice(8 * h, 8 * h + 8)
            for l in range(2):
                block = res[2 * (4 * c + h) + l, 16:24].astype(F32) * scale
                for q in range(4):
                    gka_ref[(4 * l + q) * 3 + c, rows, :] = block[:, 32 * q : 32 * q + 32]
            rest = res[24 + h, 16:24].astype(F32) * scale
            gka_ref[24 + c, rows, :] = rest[:, 32 * c : 32 * c + 32]

    for copy in departures:
        copy.wait_send()


def writer(*refs):
    sems = refs[10]
    copies = [
        pltpu.make_async_copy(src, dst, sems.at[k])
        for k, (src, dst) in enumerate(zip(refs[:5], refs[5:10]))
    ]
    for copy in copies:
        copy.start()
    for copy in copies:
        copy.wait()


def shards(n_phi, n_eta, features, cotangent, kernel_a, kernel_b, mixing):
    g1, g2 = 4 * n_eta, n_phi // 4
    assert g1 == PLANE
    cells = features.shape[1] * features.shape[2] * n_phi * n_eta
    kernel_b = jnp.swapaxes(kernel_b, 1, 2)
    ins = (features, cotangent, kernel_a, kernel_b, mixing)
    types = (BF, BF, F32, F32, F32)

    def vm(*shape, dtype=BF):
        return pltpu.VMEM(shape, dtype)

    def halo(n):
        return [vm(2 * n + 6, 32, 128)]

    dma = pltpu.SemaphoreType.DMA
    scratch = [
        *[vm(*a.shape) for a in ins], dma((5,)),
        vm(16, 32, 128), vm(2, 4, 32, 128), *halo(4),
        vm(8, 32, 128), vm(2, 2, 32, 128), *halo(2),
        vm(4, 32, 128), vm(2, 32, 128), *halo(4),
        vm(16, 32, 128), vm(2, 4, 32, 128), *halo(4),
        vm(18, 96, 128), vm(12, 96, 128), vm(10, 192, 128), vm(18, 96, 128),
        vm(16, 32, 128, dtype=F32), vm(16, 32, 128, dtype=F32), vm(10, 64, 128, dtype=F32),
        vm(8, 32, 128, dtype=F32), vm(16, 32, 128, dtype=F32),
        vm(g1, 8, 128), vm(g1 - 1, 8, 128), vm(g1, 16, 128), vm(g1 - 1, 16, 128),
        vm(24, 128), vm(g2, 24, 128), vm(24, 128), vm(g1, 24, 128),
        *[dma((4,)) for _ in range(4)],
    ]
    vmem = pl.BlockSpec(memory_space=pltpu.VMEM)
    anywhere = pl.BlockSpec(memory_space=pl.ANY)
    shapes = [a.shape for a in ins]
    outs = pl.pallas_call(
        functools.partial(kernel, n_phi, n_eta, 1.0 / math.sqrt(cells)),
        out_shape=tuple(pltpu.VMEM(s, t) for s, t in zip(shapes, types)),
        in_specs=[anywhere] * 5,
        out_specs=(vmem,) * 5,
        scratch_shapes=scratch,
        compiler_params=pltpu.CompilerParams(collective_id=0, has_side_effects=True),
        name="block_step",
    )(*ins)
    outs = pl.pallas_call(
        writer,
        out_shape=tuple(jax.ShapeDtypeStruct(s, t) for s, t in zip(shapes, types)),
        in_specs=[vmem] * 5,
        out_specs=(anywhere,) * 5,
        scratch_shapes=[dma((5,))],
        name="write_out",
    )(*[pltpu.with_memory_space_constraint(o, pltpu.VMEM) for o in outs])
    return (*outs[:3], jnp.swapaxes(outs[3], 1, 2), outs[4])


def solution(mesh):
    specs = (P(None, "phi", "eta"), P(None, "phi", "eta"), P(), P(), P())
    body = functools.partial(shards, mesh.shape["phi"], mesh.shape["eta"])
    return jax.shard_map(body, mesh=mesh, in_specs=specs, out_specs=specs, check_vma=False)
```

time: 52.7 us -> 42.5 us (0.81)
  local copies, waits for them, and re-layouts: 6.85 us -> 0 us
  Pallas kernels: 45 us -> 41.8 us
    unnamed x13 -> x0, local copies, waits for them, and re-layouts: 4.59 us -> none
    pallas_call x1, Pallas kernels: 45 us -> 40.7 us  [shards(): pl.pallas_call(functools.partial(kernel, n_phi, n_eta, 1.0 / math.sqrt(ce...]
    pallas_call x1 -> x0, local copies, waits for them, and re-layouts: 2.26 us -> none  [shards(): pl.pallas_call(functools.partial(kernel, n_phi, n_eta, 1.0 / math.sqrt(ce...]
    pallas_call x0 -> x1, Pallas kernels: none -> 1.04 us  [shards(): pl.pallas_call(writer, out_shape=tuple((jax.ShapeDtypeStruct(s, t) for s,...]
where the time goes in v2:
time: 42.5 us; the launch traced here: 42.4 us
  Pallas kernels  41.8 us (98%)
  between operations  0.64 us (2%)
    pallas_call x1, Pallas kernels, shards(): pl.pallas_call(functools.partial(kernel, n_phi, n_eta, 1.0 / math.sqrt(ce...  40.7 us
    pallas_call x1, Pallas kernels, shards(): pl.pallas_call(writer, out_shape=tuple((jax.ShapeDtypeStruct(s, t) for s,...  1.04 us

profile of v2, /device:TPU:1, one launch (start us, length us, event | category | flops | bytes accessed | tf_op | source)
XLA Modules:
  0.0 42.4 jit_solution(11175615888123610679)
XLA Ops:
  0.6 40.7 %block_step.1 = (bf16[32,16,128]{2,1,0:T(8,128)(2,1)S(1)}, bf16[32,16,128]{2,1,0:T(8,128)(2,1)S(1)}, f32[27,32,32]{2,1,0:T(8,128)S(1)}, f32[27,32,64]{2,1,0:T(8,128)S(1)}, f32[32,64]{1,0:T(8,128)S(1)}) custom-call(bf16[32,16,128]{2,1,0:T(8,128)(2,1)} %refs_0_.1, bf16[32,16,128]{2,1,0:T(8,128)(2,1)} %refs_1_.1, bf16[27,32,32]{2,1,0:T(8,128)(2,1)} %refs_2_.1, ...), custom_call_target="tpu_custom_call" | custom-call | tf_op jit(solution)/shard_map/block_step/pallas_call | solution.py:486
  41.4 1.0 %write_out.1 = (bf16[32,16,128]{2,1,0:T(8,128)(2,1)}, bf16[32,16,128]{2,1,0:T(8,128)(2,1)}, f32[27,32,32]{2,1,0:T(8,128)}, f32[27,32,64]{2,1,0:T(8,128)}, f32[32,64]{1,0:T(8,128)}) custom-call(bf16[32,16,128]{2,1,0:T(8,128)(2,1)S(1)} %get-tuple-element.15.refs_0_, bf16[32,16,128]{2,1,0:T(8,128)(2,1)S(1)} %get-tuple-element.16.refs_1_, ...), custom_call_target="tpu_custom_call" | custom-call | tf_op jit(solution)/shard_map/write_out/pallas_call | solution.py:495

commit v3 on v2

--- a/solution.py
+++ b/solution.py
@@ -61,9 +61,10 @@
     return jnp.where(lane_of(x.shape) < 64, roll(x, -32), roll(y, 32))
 
 
-def widen_columns(x):
-    lane = lane_of(x.shape)
-    return jnp.where(lane < 32, roll(x, -32), jnp.where(lane < 96, x, roll(x, 32)))
+def widen_pairs(x):
+    up, down, across = roll(x, 32), roll(x, -32), roll(x, 64)
+    low, high = by_quarter(x, up, up, across), by_quarter(across, down, down, x)
+    return jnp.concatenate([low, high], axis=0)
 
 
 def pool_columns(x):
@@ -106,8 +107,8 @@
         fold_s, colf_s, rf,
         colc_s, rowc_s, rc,
         g_s, colg_s, rg,
-        sfa, scb, sgb, sga, slope_a_s, lin_a_s, lin_b_s, gc_s, gi_s,
-        pa, ra, pb, rb, x2, r2, x3, res,
+        sfa, sft, scb, sgb, sga, slope_a_s, lin_a_s, lin_b_s, gc_s, gi_s,
+        pa, ra, xa2, ra2, xa3, resa, pb, rb, xb2, rb2, xb3, resb,
         h_send, h_recv, s_send, s_recv,
     ) = refs[10:]
     p = lax.axis_index("phi")
@@ -131,9 +132,9 @@
         return (r * 4 + lax.rem(p, 4), e)
 
     barrier = pltpu.get_barrier_semaphore()
-    targets = [line_device(i) for i in sorted(range(1, g2), key=lambda i: -min(i, g2 - i))]
+    targets = [halo_device(d) for d in DIRS]
+    targets += [line_device(i) for i in sorted(range(1, g2), key=lambda i: -min(i, g2 - i))]
     targets += [plane_device(i) for i in range(1, g1)]
-    targets += [halo_device(d) for d in DIRS]
     for target in targets:
         pl.semaphore_signal(barrier, inc=1, device_id=target, device_id_type=MESH)
 
@@ -161,7 +162,7 @@
     def halo_start(which, cols, rows, arrived):
         n = (arrived.shape[0] - 6) // 2
         ssem, rsem = h_send.at[which], h_recv.at[which]
-        for k, d in enumerate(DIRS):
+        for k, d in sorted(enumerate(DIRS), key=lambda kd: -abs(kd[1][0]) - abs(kd[1][1])):
             if k < 2:
                 src, dst = cols[k], arrived.at[pl.ds(n * k, n)]
             else:
@@ -224,26 +225,34 @@
     mix = mix_ref[...]
     mix_t = mix.T
 
-    def fine_windows(dst, middle, arrived):
+    def fine_windows_own(dst, rows):
+        lane = lane_of(rows.shape)
+        dst[1:17, 0:32, :] = jnp.where(lane < 32, zero(rows), roll(rows, 32))
+        dst[1:17, 32:64, :] = rows
+        dst[1:17, 64:96, :] = jnp.where(lane >= 96, zero(rows), roll(rows, -32))
+
+    def fine_windows_rim(dst, arrived):
         cols, rim = halo_parts(arrived)
-        rows = jnp.concatenate([rim[0], middle, rim[3]], axis=0)
-        left = jnp.concatenate(
-            [roll(rim[1], 32)] + unpack_column(cols[0], 0) + [roll(rim[4], 32)], axis=0
-        )
-        right = jnp.concatenate(
-            [roll(rim[2], 96)] + unpack_column(cols[1], 96) + [roll(rim[5], 96)], axis=0
-        )
-        lane = lane_of(rows.shape)
-        dst[:, 0:32, :] = jnp.where(
-            lane < lo32, left, jnp.where(lane < 32, zero(rows), roll(rows, 32))
-        )
-        dst[:, 32:64, :] = rows
-        dst[:, 64:96, :] = jnp.where(
-            lane >= hi96, right, jnp.where(lane >= 96, zero(rows), roll(rows, -32))
-        )
+        lane = lane_of((16, 32, 128))
+        left = jnp.concatenate(unpack_column(cols[0], 0), axis=0)
+        right = jnp.concatenate(unpack_column(cols[1], 96), axis=0)
+        dst[1:17, 0:32, :] = jnp.where(lane < lo32, left, dst[1:17, 0:32, :])
+        dst[1:17, 64:96, :] = jnp.where(lane >= hi96, right, dst[1:17, 64:96, :])
+        lane = lane_of((1, 32, 128))
+        for k, at in ((0, 0), (3, 17)):
+            rows, left, right = rim[k], roll(rim[k + 1], 32), roll(rim[k + 2], 96)
+            dst[at : at + 1, 0:32, :] = jnp.where(
+                lane < lo32, left, jnp.where(lane < 32, zero(rows), roll(rows, 32))
+            )
+            dst[at : at + 1, 32:64, :] = rows
+            dst[at : at + 1, 64:96, :] = jnp.where(
+                lane >= hi96, right, jnp.where(lane >= 96, zero(rows), roll(rows, -32))
+            )
+
+    fine_windows_own(sfa, x)
 
     halo_x.wait_recv()
-    fine_windows(sfa, x, rx)
+    fine_windows_rim(sfa, rx)
     conv_rows(sfa, 16, wa_f, 32, lin_a_s)
     lin_a = lin_a_s[...]
     hidden = (lin_a / (1.0 + jnp.exp(-lin_a))).astype(BF).astype(F32).reshape(8, 2, 32, 128)
@@ -272,32 +281,45 @@
         ),
     )
 
+    fold_pairs = pack_pair(fold[0:4], fold[4:8])
     grad_gated = dot(mix_t, side_by_side([fold_wide[r] for r in range(10)]))
     sig_a = sigmoid(lin_a)
     slope_a_s[...] = sig_a * (1.0 + lin_a * (1.0 - sig_a))
 
+    own_rows = slice(2, 10)
+    lane = lane_of(coarse.shape)
+    scb[own_rows, 0:32, :] = jnp.where(lane < 64, zero(coarse), roll(coarse, 32))
+    scb[own_rows, 32:64, :] = coarse
+    scb[own_rows, 64:96, :] = jnp.where(lane < 64, roll(coarse, -32), zero(coarse))
+
+    for r in range(16):
+        sft[r] = sfa[r : r + 3].reshape(288, 128).T
+
     halo_c.wait_recv()
     cols, rim = halo_parts(rc)
-    rows = jnp.concatenate(
-        [roll(rim[0], 32), roll(rim[0], -32), coarse, roll(rim[3], 32), roll(rim[3], -32)],
-        axis=0,
-    )
-    left = jnp.concatenate(
-        [rim[1], roll(rim[1], 64), cols[0], roll(cols[0], 64), rim[4], roll(rim[4], 64)],
-        axis=0,
-    )
-    right = jnp.concatenate(
-        [roll(rim[2], 64), rim[2], roll(cols[1], 64), cols[1], roll(rim[5], 64), rim[5]],
-        axis=0,
-    )
-    lane = lane_of(rows.shape)
+
+    def two(*parts):
+        return jnp.concatenate(parts, axis=0)
+
+    left, right = two(cols[0], roll(cols[0], 64)), two(roll(cols[1], 64), cols[1])
     left = jnp.where(lane < lo64, left, zero(left))
     right = jnp.where(lane >= hi64, right, zero(right))
-    scb[:, 0:32, :] = jnp.where(lane < 64, left, roll(rows, 32))
-    scb[:, 32:64, :] = jnp.where(
-        lane < 32, roll(left, -32), jnp.where(lane < 96, rows, roll(right, 32))
-    )
-    scb[:, 64:96, :] = jnp.where(lane < 64, roll(rows, -32), right)
+    scb[own_rows, 0:32, :] = jnp.where(lane < 64, left, scb[own_rows, 0:32, :])
+    scb[own_rows, 32:64, :] = jnp.where(
+        lane < 32, roll(left, -32), jnp.where(lane < 96, coarse, roll(right, 32))
+    )
+    scb[own_rows, 64:96, :] = jnp.where(lane < 64, scb[own_rows, 64:96, :], right)
+    lane = lane_of((2, 32, 128))
+    for k, at in ((0, 0), (3, 10)):
+        rows = two(roll(rim[k], 32), roll(rim[k], -32))
+        left, right = two(rim[k + 1], roll(rim[k + 1], 64)), two(roll(rim[k + 2], 64), rim[k + 2])
+        left = jnp.where(lane < lo64, left, zero(left))
+        right = jnp.where(lane >= hi64, right, zero(right))
+        scb[at : at + 2, 0:32, :] = jnp.where(lane < 64, left, roll(rows, 32))
+        scb[at : at + 2, 32:64, :] = jnp.where(
+            lane < 32, roll(left, -32), jnp.where(lane < 96, rows, roll(right, 32))
+        )
+        scb[at : at + 2, 64:96, :] = jnp.where(lane < 64, roll(rows, -32), right)
 
     conv_rows(scb, 10, wb_f, 64, lin_b_s)
     lin_b = lin_b_s[...]
@@ -308,19 +330,20 @@
         [(grad_gated[:, 128 * r : 128 * (r + 1)] * slope_b[r]).astype(BF)[None] for r in range(10)],
         axis=0,
     )
-    sgb[:, 0:64, :] = roll(grad_b, 32)
-    sgb[:, 64:128, :] = grad_b
-    sgb[:, 128:192, :] = roll(grad_b, -32)
-
-    own = grad_b[1:9]
-    lane = lane_of(own.shape)
-    own = jnp.where((lane >= 32) & (lane < 96), own, zero(own))
-    shifts = layer_shifts(own)
-    up = side_by_side([jnp.concatenate([s[r] for s in shifts], axis=0) for r in range(8)])
-    seen = side_by_side([scb[r + 1 : r + 4].reshape(288, 128) for r in range(8)])
+    top, low = grad_b[0:6], grad_b[4:10]
+    lane = lane_of(top.shape)
+    sgb[:, 0:64, :] = jnp.where(lane < 64, top, roll(low, 64))
+    sgb[:, 64:128, :] = pack_pair(top, low)
+    sgb[:, 128:192, :] = jnp.where(lane < 64, roll(top, 64), low)
+
+    shifts = layer_shifts(sgb[1:5, 64:128, :])
+    up = side_by_side([jnp.concatenate([s[r] for s in shifts], axis=0) for r in range(4)])
+    seen = pack_pair(scb[1:7], scb[5:11])
+    seen = side_by_side([seen[r : r + 3].reshape(288, 128) for r in range(4)])
+    gated = pack_pair(gated[0:4], gated[4:8])
     sum_b = dot_nt(seen, up)
     sum_m = dot_nt(
-        side_by_side([fold[r] for r in range(8)]), side_by_side([gated[r] for r in range(8)])
+        side_by_side([fold_pairs[r] for r in range(4)]), side_by_side([gated[r] for r in range(4)])
     )
     for i in range(18):
         pb[i] = sum_b[16 * i : 16 * i + 16, 0:128].astype(BF)
@@ -341,19 +364,16 @@
 
     spread_b = spread(pb, rb, 0)
 
-    conv_rows(sgb, 8, wb_b, 32, gc_s)
-    grad_coarse = widen_columns(gc_s[...].astype(BF).astype(F32))
+    conv_rows(sgb, 4, wb_b, 32, gc_s)
+    grad_coarse = widen_pairs(gc_s[...].astype(BF).astype(F32))
     grad_hidden = jnp.concatenate(
         [(ct[:, i] + 0.25 * grad_coarse)[:, None] for i in range(2)], axis=1
     ).reshape(16, 32, 128)
     grad_a = (grad_hidden * slope_a_s[...]).astype(BF)
     g_s[...] = grad_a
-    colg_s[0] = pack_column(grad_a, 4, 96)
-    colg_s[1] = pack_column(grad_a, 4, 0)
     shifts = layer_shifts(grad_a)
     up = side_by_side([jnp.concatenate([s[r] for s in shifts], axis=0) for r in range(16)])
-    seen = side_by_side([sfa[r : r + 3].reshape(288, 128) for r in range(16)])
-    sum_a = dot_nt(up, seen)
+    sum_a = dot(up, sft[...].reshape(2048, 288))
     for i in range(12):
         for l in range(2):
             pa[2 * i + l] = sum_a[8 * i : 8 * i + 8, 128 * l : 128 * l + 128].astype(BF)
@@ -364,76 +384,85 @@
     for t in range(28, PLANE):
         pa[t] = jnp.zeros((8, 128), BF)
     spread_a = spread(pa, ra, 1)
-    projected = dot(mix, side_by_side([gated[r] for r in range(8)])).astype(BF).astype(F32)
+    colg_s[0] = pack_column(grad_a, 4, 96)
+    colg_s[1] = pack_column(grad_a, 4, 0)
+    projected = dot(mix, side_by_side([gated[r] for r in range(4)])).astype(BF).astype(F32)
     projected = jnp.concatenate(
-        [projected[:, 128 * r : 128 * (r + 1)][None] for r in range(8)], axis=0
-    )
-    projected = widen_columns(projected)
+        [projected[:, 128 * r : 128 * (r + 1)][None] for r in range(4)], axis=0
+    )
+    projected = widen_pairs(projected)
     output = jnp.concatenate(
         [(hidden[:, i] + projected)[:, None] for i in range(2)], axis=1
     ).reshape(16, 32, 128)
     out_ref[...] = jnp.transpose(output.astype(BF), (1, 0, 2))
 
-    spread_b.wait_recv()
-    total_b = pb[me1].astype(F32)
-    for i in range(g1 - 1):
-        total_b = total_b + rb[i].astype(F32)
-    spread_a.wait_recv()
-    total_a = pa[me1].astype(F32)
-    for i in range(g1 - 1):
-        total_a = total_a + ra[i].astype(F32)
-    total = jnp.concatenate([total_b, total_a], axis=0).astype(BF)
-    x2[...] = total
-    r2[me2] = total
-    for i in range(1, g2):
-        send(x2, r2.at[me2], s_send.at[2], s_recv.at[2], line_device(i))
-    crossed = whole(r2.at[pl.ds(0, g2 - 1)], s_send.at[2], s_recv.at[2])
-    departures.append(crossed)
-
+    def cross(copy, buf, arrived, mine, slots, k):
+        copy.wait_recv()
+        total = buf[me1].astype(F32)
+        for i in range(g1 - 1):
+            total = total + arrived[i].astype(F32)
+        total = total.astype(BF)
+        mine[...] = total
+        slots[me2] = total
+        for i in range(1, g2):
+            send(mine, slots.at[me2], s_send.at[k], s_recv.at[k], line_device(i))
+        copy = whole(slots.at[pl.ds(0, g2 - 1)], s_send.at[k], s_recv.at[k])
+        departures.append(copy)
+        return copy
+
+    def gather(copy, slots, mine, result, k):
+        copy.wait_recv()
+        total = slots[0].astype(F32)
+        for i in range(1, g2):
+            total = total + slots[i].astype(F32)
+        total = total.astype(BF)
+        mine[...] = total
+        result[me1] = total
+        for i in range(1, g1):
+            send(mine, result.at[me1], s_send.at[k], s_recv.at[k], plane_device(i))
+        copy = whole(result.at[pl.ds(0, g1 - 1)], s_send.at[k], s_recv.at[k])
+        departures.append(copy)
+        return copy
+
+    cross_b = cross(spread_b, pb, rb, xb2, rb2, 2)
+    cross_a = cross(spread_a, pa, ra, xa2, ra2, 3)
     halo_g = halo_start(
         3, (colg_s.at[0], colg_s.at[1]), (g_s.at[15], g_s.at[0]), rg
     )
 
-    crossed.wait_recv()
-    total = r2[0].astype(F32)
-    for i in range(1, g2):
-        total = total + r2[i].astype(F32)
-    total = total.astype(BF)
-    x3[...] = total
-    res[me1] = total
-    for i in range(1, g1):
-        send(x3, res.at[me1], s_send.at[3], s_recv.at[3], plane_device(i))
-    gathered = whole(res.at[pl.ds(0, g1 - 1)], s_send.at[3], s_recv.at[3])
-    departures.append(gathered)
+    gather_b = gather(cross_b, rb2, xb3, resb, 4)
+    gather_a = gather(cross_a, ra2, xa3, resa, 5)
+
+    fine_windows_own(sga, grad_a)
     halo_g.wait_recv()
-    fine_windows(sga, grad_a, rg)
+    fine_windows_rim(sga, rg)
     conv_rows(sga, 16, wa_b, 32, gi_s)
     gi_ref[...] = jnp.transpose(gi_s[...].astype(BF), (1, 0, 2))
 
-    gathered.wait_recv()
-
+    gather_b.wait_recv()
     for ab in range(9):
         for h in range(2):
             rows = slice(16 * h, 16 * h + 16)
             u = 2 * ab + h
-            pair = res[u, 0:16].astype(F32) * scale
+            pair = resb[u].astype(F32) * scale
             gkb_ref[3 * ab, rows, :] = pair[:, 0:64]
             gkb_ref[3 * ab + 1, rows, :] = pair[:, 64:128]
             g = u // 9
-            rest = res[18 + u % 9, 0:16].astype(F32) * scale
+            rest = resb[18 + u % 9].astype(F32) * scale
             gkb_ref[3 * ab + 2, rows, :] = rest[:, 64 * g : 64 * g + 64]
-    last = res[27, 0:16].astype(F32) * scale
+    last = resb[27].astype(F32) * scale
     gm_ref[0:16, :] = last[:, 0:64]
     gm_ref[16:32, :] = last[:, 64:128]
 
+    gather_a.wait_recv()
     for c in range(3):
         for h in range(4):
             rows = slice(8 * h, 8 * h + 8)
             for l in range(2):
-                block = res[2 * (4 * c + h) + l, 16:24].astype(F32) * scale
+                block = resa[2 * (4 * c + h) + l].astype(F32) * scale
                 for q in range(4):
                     gka_ref[(4 * l + q) * 3 + c, rows, :] = block[:, 32 * q : 32 * q + 32]
-            rest = res[24 + h, 16:24].astype(F32) * scale
+            rest = resa[24 + h].astype(F32) * scale
             gka_ref[24 + c, rows, :] = rest[:, 32 * c : 32 * c + 32]
 
     for copy in departures:
@@ -441,11 +470,15 @@
 
 
 def writer(*refs):
-    sems = refs[10]
-    copies = [
-        pltpu.make_async_copy(src, dst, sems.at[k])
-        for k, (src, dst) in enumerate(zip(refs[:5], refs[5:10]))
-    ]
+    sems, copies = refs[10], []
+    for src, dst in zip(refs[:5], refs[5:10]):
+        parts = 3 if src.shape[0] == 27 else 1
+        rows = src.shape[0] // parts
+        for i in range(parts):
+            at = pl.ds(i * rows, rows)
+            copies.append(
+                pltpu.make_async_copy(src.at[at], dst.at[at], sems.at[len(copies)])
+            )
     for copy in copies:
         copy.start()
     for copy in copies:
@@ -463,6 +496,12 @@
     def vm(*shape, dtype=BF):
         return pltpu.VMEM(shape, dtype)
 
+    def sums(n):
+        return [
+            vm(g1, n, 128), vm(g1 - 1, n, 128), vm(n, 128),
+            vm(g2, n, 128), vm(n, 128), vm(g1, n, 128),
+        ]
+
     def halo(n):
         return [vm(2 * n + 6, 32, 128)]
 
@@ -473,12 +512,11 @@
         vm(8, 32, 128), vm(2, 2, 32, 128), *halo(2),
         vm(4, 32, 128), vm(2, 32, 128), *halo(4),
         vm(16, 32, 128), vm(2, 4, 32, 128), *halo(4),
-        vm(18, 96, 128), vm(12, 96, 128), vm(10, 192, 128), vm(18, 96, 128),
+        vm(18, 96, 128), vm(16, 128, 288), vm(12, 96, 128), vm(6, 192, 128), vm(18, 96, 128),
         vm(16, 32, 128, dtype=F32), vm(16, 32, 128, dtype=F32), vm(10, 64, 128, dtype=F32),
-        vm(8, 32, 128, dtype=F32), vm(16, 32, 128, dtype=F32),
-        vm(g1, 8, 128), vm(g1 - 1, 8, 128), vm(g1, 16, 128), vm(g1 - 1, 16, 128),
-        vm(24, 128), vm(g2, 24, 128), vm(24, 128), vm(g1, 24, 128),
-        *[dma((4,)) for _ in range(4)],
+        vm(4, 32, 128, dtype=F32), vm(16, 32, 128, dtype=F32),
+        *sums(8), *sums(16),
+        *[dma((k,)) for k in (4, 4, 6, 6)],
     ]
     vmem = pl.BlockSpec(memory_space=pltpu.VMEM)
     anywhere = pl.BlockSpec(memory_space=pl.ANY)
@@ -497,7 +535,7 @@
         out_shape=tuple(jax.ShapeDtypeStruct(s, t) for s, t in zip(shapes, types)),
         in_specs=[vmem] * 5,
         out_specs=(anywhere,) * 5,
-        scratch_shapes=[dma((5,))],
+        scratch_shapes=[dma((9,))],
         name="write_out",
     )(*[pltpu.with_memory_space_constraint(o, pltpu.VMEM) for o in outs])
     return (*outs[:3], jnp.swapaxes(outs[3], 1, 2), outs[4])

time: 42.5 us -> 41.3 us (0.972)
  Pallas kernels: 41.8 us -> 40.6 us
    pallas_call x1, Pallas kernels: 40.7 us -> 39.5 us  [shards(): pl.pallas_call(functools.partial(kernel, n_phi, n_eta, 1.0 / math.sqrt(ce...]
where the time goes in v3:
time: 41.3 us; the launch traced here: 41.2 us
  Pallas kernels  40.6 us (98%)
  between operations  0.64 us (2%)
    pallas_call x1, Pallas kernels, shards(): pl.pallas_call(functools.partial(kernel, n_phi, n_eta, 1.0 / math.sqrt(ce...  39.5 us
    pallas_call x1, Pallas kernels, shards(): pl.pallas_call(writer, out_shape=tuple((jax.ShapeDtypeStruct(s, t) for s,...  1.07 us

profile of v3, /device:TPU:1, one launch (start us, length us, event | category | flops | bytes accessed | tf_op | source)
XLA Modules:
  0.0 41.2 jit_solution(5084077982359704174)
XLA Ops:
  0.6 39.5 %block_step.1 = (bf16[32,16,128]{2,1,0:T(8,128)(2,1)S(1)}, bf16[32,16,128]{2,1,0:T(8,128)(2,1)S(1)}, f32[27,32,32]{2,1,0:T(8,128)S(1)}, f32[27,32,64]{2,1,0:T(8,128)S(1)}, f32[32,64]{1,0:T(8,128)S(1)}) custom-call(bf16[32,16,128]{2,1,0:T(8,128)(2,1)} %refs_0_.1, bf16[32,16,128]{2,1,0:T(8,128)(2,1)} %refs_1_.1, bf16[27,32,32]{2,1,0:T(8,128)(2,1)} %refs_2_.1, ...), custom_call_target="tpu_custom_call" | custom-call | tf_op jit(solution)/shard_map/block_step/pallas_call | solution.py:524
  40.1 1.1 %write_out.1 = (bf16[32,16,128]{2,1,0:T(8,128)(2,1)}, bf16[32,16,128]{2,1,0:T(8,128)(2,1)}, f32[27,32,32]{2,1,0:T(8,128)}, f32[27,32,64]{2,1,0:T(8,128)}, f32[32,64]{1,0:T(8,128)}) custom-call(bf16[32,16,128]{2,1,0:T(8,128)(2,1)S(1)} %get-tuple-element.15.refs_0_, bf16[32,16,128]{2,1,0:T(8,128)(2,1)S(1)} %get-tuple-element.16.refs_1_, ...), custom_call_target="tpu_custom_call" | custom-call | tf_op jit(solution)/shard_map/write_out/pallas_call | solution.py:533

commit v4 on v3

--- a/solution.py
+++ b/solution.py
@@ -114,35 +114,43 @@
     p = lax.axis_index("phi")
     e = lax.axis_index("eta")
     g1, g2 = 4 * n_eta, n_phi // 4
-    me1 = lax.rem(p, 4) * n_eta + e
     me2 = p // 4
 
     def wrap(i, n):
         return jnp.where(i >= n, i - n, i)
 
+    in_plane = lax.rem(p, 4)
+    plane_p = [wrap(in_plane + i, 4) for i in range(4)]
+    phi_of = [me2 * 4 + i for i in plane_p]
+    eta_of = [wrap(e + i, n_eta) for i in range(n_eta)]
+    line_of = [wrap(p + 4 * i, n_phi) for i in range(g2)]
+    near_of = {0: p, 1: wrap(p + 1, n_phi), -1: wrap(p + n_phi - 1, n_phi)}
+    me1 = in_plane * n_eta + e
+    steps = [(i, j) for i in range(4) for j in range(n_eta) if i or j]
+    steps.sort(key=lambda ij: (-min(ij[1], n_eta - ij[1]), -min(ij[0], 4 - ij[0])))
+
     def halo_device(d):
-        return (wrap(p + d[0] % n_phi, n_phi), wrap(e + d[1] % n_eta, n_eta))
-
-    def plane_device(i):
-        q = wrap(me1 + i, g1)
-        return (me2 * 4 + q // n_eta, lax.rem(q, n_eta))
+        return (near_of[d[0]], eta_of[d[1] % n_eta])
+
+    def plane_device(step):
+        return (phi_of[step[0]], eta_of[step[1]])
 
     def line_device(i):
-        r = wrap(me2 + i, g2)
-        return (r * 4 + lax.rem(p, 4), e)
-
-    barrier = pltpu.get_barrier_semaphore()
-    targets = [halo_device(d) for d in DIRS]
-    targets += [line_device(i) for i in sorted(range(1, g2), key=lambda i: -min(i, g2 - i))]
-    targets += [plane_device(i) for i in range(1, g1)]
-    for target in targets:
-        pl.semaphore_signal(barrier, inc=1, device_id=target, device_id_type=MESH)
+        return (line_of[i], e)
 
     loads = [
         pltpu.make_async_copy(src, dst, load_sem.at[k])
         for k, (src, dst) in enumerate(zip(ins, (f_ref, ct_ref, ka_ref, kb_ref, mix_ref)))
     ]
-    for load in loads:
+    loads[0].start()
+
+    barrier = pltpu.get_barrier_semaphore()
+    targets = [line_device(i) for i in sorted(range(1, g2), key=lambda i: -min(i, g2 - i))]
+    planes = [plane_device(step) for step in steps]
+    targets += planes[:12] + [halo_device(d) for d in DIRS] + planes[12:]
+    for target in targets:
+        pl.semaphore_signal(barrier, inc=1, device_id=target, device_id_type=MESH)
+    for load in loads[1:]:
         load.start()
 
     departures = []
@@ -355,9 +363,9 @@
         pb[t] = jnp.zeros((16, 128), BF)
 
     def spread(buf, dst, k):
-        for i in range(1, g1):
-            q = wrap(me1 + i, g1)
-            send(buf.at[q], dst.at[i - 1], s_send.at[k], s_recv.at[k], plane_device(i))
+        for i, step in enumerate(steps):
+            q = plane_p[step[0]] * n_eta + eta_of[step[1]]
+            send(buf.at[q], dst.at[i], s_send.at[k], s_recv.at[k], plane_device(step))
         copy = whole(dst, s_send.at[k], s_recv.at[k])
         departures.append(copy)
         return copy
@@ -418,8 +426,8 @@
         total = total.astype(BF)
         mine[...] = total
         result[me1] = total
-        for i in range(1, g1):
-            send(mine, result.at[me1], s_send.at[k], s_recv.at[k], plane_device(i))
+        for step in steps:
+            send(mine, result.at[me1], s_send.at[k], s_recv.at[k], plane_device(step))
         copy = whole(result.at[pl.ds(0, g1 - 1)], s_send.at[k], s_recv.at[k])
         departures.append(copy)
         return copy

time: 41.3 us -> 40.5 us (0.981)
  Pallas kernels: 40.6 us -> 39.8 us
    pallas_call x1, Pallas kernels: 39.5 us -> 38.7 us  [shards(): pl.pallas_call(functools.partial(kernel, n_phi, n_eta, 1.0 / math.sqrt(ce...]
where the time goes in v4:
time: 40.5 us; the launch traced here: 40.4 us
  Pallas kernels  39.8 us (98%)
  between operations  0.64 us (2%)
    pallas_call x1, Pallas kernels, shards(): pl.pallas_call(functools.partial(kernel, n_phi, n_eta, 1.0 / math.sqrt(ce...  38.7 us
    pallas_call x1, Pallas kernels, shards(): pl.pallas_call(writer, out_shape=tuple((jax.ShapeDtypeStruct(s, t) for s,...  1.07 us

profile of v4, /device:TPU:1, one launch (start us, length us, event | category | flops | bytes accessed | tf_op | source)
XLA Modules:
  0.0 40.4 jit_solution(17751554412242998751)
XLA Ops:
  0.6 38.7 %block_step.1 = (bf16[32,16,128]{2,1,0:T(8,128)(2,1)S(1)}, bf16[32,16,128]{2,1,0:T(8,128)(2,1)S(1)}, f32[27,32,32]{2,1,0:T(8,128)S(1)}, f32[27,32,64]{2,1,0:T(8,128)S(1)}, f32[32,64]{1,0:T(8,128)S(1)}) custom-call(bf16[32,16,128]{2,1,0:T(8,128)(2,1)} %refs_0_.1, bf16[32,16,128]{2,1,0:T(8,128)(2,1)} %refs_1_.1, bf16[27,32,32]{2,1,0:T(8,128)(2,1)} %refs_2_.1, ...), custom_call_target="tpu_custom_call" | custom-call | tf_op jit(solution)/shard_map/block_step/pallas_call | solution.py:532
  39.3 1.1 %write_out.1 = (bf16[32,16,128]{2,1,0:T(8,128)(2,1)}, bf16[32,16,128]{2,1,0:T(8,128)(2,1)}, f32[27,32,32]{2,1,0:T(8,128)}, f32[27,32,64]{2,1,0:T(8,128)}, f32[32,64]{1,0:T(8,128)}) custom-call(bf16[32,16,128]{2,1,0:T(8,128)(2,1)S(1)} %get-tuple-element.15.refs_0_, bf16[32,16,128]{2,1,0:T(8,128)(2,1)S(1)} %get-tuple-element.16.refs_1_, ...), custom_call_target="tpu_custom_call" | custom-call | tf_op jit(solution)/shard_map/write_out/pallas_call | solution.py:541

commit v5 on v4

--- a/solution.py
+++ b/solution.py
@@ -209,9 +209,6 @@
     fold_s[...] = fold
     colf_s[0] = pack_column(fold, 2, 64)
     colf_s[1] = pack_column(fold, 2, 32)
-    halo_f = halo_start(
-        1, (colf_s.at[0], colf_s.at[1]), (fold_s.at[7], fold_s.at[0]), rf
-    )
 
     def forward_weight(ref):
         return jnp.concatenate(
@@ -259,6 +256,11 @@
 
     fine_windows_own(sfa, x)
 
+    halo_x.wait_send()
+    departures.remove(halo_x)
+    halo_f = halo_start(
+        1, (colf_s.at[0], colf_s.at[1]), (fold_s.at[7], fold_s.at[0]), rf
+    )
     halo_x.wait_recv()
     fine_windows_rim(sfa, rx)
     conv_rows(sfa, 16, wa_f, 32, lin_a_s)
@@ -478,15 +480,11 @@
 
 
 def writer(*refs):
-    sems, copies = refs[10], []
-    for src, dst in zip(refs[:5], refs[5:10]):
-        parts = 3 if src.shape[0] == 27 else 1
-        rows = src.shape[0] // parts
-        for i in range(parts):
-            at = pl.ds(i * rows, rows)
-            copies.append(
-                pltpu.make_async_copy(src.at[at], dst.at[at], sems.at[len(copies)])
-            )
+    sems = refs[10]
+    copies = [
+        pltpu.make_async_copy(src, dst, sems.at[k])
+        for k, (src, dst) in enumerate(zip(refs[:5], refs[5:10]))
+    ]
     for copy in copies:
         copy.start()
     for copy in copies:
@@ -543,7 +541,7 @@
         out_shape=tuple(jax.ShapeDtypeStruct(s, t) for s, t in zip(shapes, types)),
         in_specs=[vmem] * 5,
         out_specs=(anywhere,) * 5,
-        scratch_shapes=[dma((9,))],
+        scratch_shapes=[dma((5,))],
         name="write_out",
     )(*[pltpu.with_memory_space_constraint(o, pltpu.VMEM) for o in outs])
     return (*outs[:3], jnp.swapaxes(outs[3], 1, 2), outs[4])

time: 40.5 us -> 40.3 us (level)
  no operation moved by 1% of the time
where the time goes in v5:
time: 40.3 us; the launch traced here: 40.2 us
  Pallas kernels  39.6 us (98%)
  between operations  0.64 us (2%)
    pallas_call x1, Pallas kernels, shards(): pl.pallas_call(functools.partial(kernel, n_phi, n_eta, 1.0 / math.sqrt(ce...  38.5 us
    pallas_call x1, Pallas kernels, shards(): pl.pallas_call(writer, out_shape=tuple((jax.ShapeDtypeStruct(s, t) for s,...  1.04 us

profile of v5, /device:TPU:1, one launch (start us, length us, event | category | flops | bytes accessed | tf_op | source)
XLA Modules:
  0.0 40.2 jit_solution(14465176824095653464)
XLA Ops:
  0.6 38.5 %block_step.1 = (bf16[32,16,128]{2,1,0:T(8,128)(2,1)S(1)}, bf16[32,16,128]{2,1,0:T(8,128)(2,1)S(1)}, f32[27,32,32]{2,1,0:T(8,128)S(1)}, f32[27,32,64]{2,1,0:T(8,128)S(1)}, f32[32,64]{1,0:T(8,128)S(1)}) custom-call(bf16[32,16,128]{2,1,0:T(8,128)(2,1)} %refs_0_.1, bf16[32,16,128]{2,1,0:T(8,128)(2,1)} %refs_1_.1, bf16[27,32,32]{2,1,0:T(8,128)(2,1)} %refs_2_.1, ...), custom_call_target="tpu_custom_call" | custom-call | tf_op jit(solution)/shard_map/block_step/pallas_call | solution.py:530
  39.2 1.0 %write_out.1 = (bf16[32,16,128]{2,1,0:T(8,128)(2,1)}, bf16[32,16,128]{2,1,0:T(8,128)(2,1)}, f32[27,32,32]{2,1,0:T(8,128)}, f32[27,32,64]{2,1,0:T(8,128)}, f32[32,64]{1,0:T(8,128)}) custom-call(bf16[32,16,128]{2,1,0:T(8,128)(2,1)S(1)} %get-tuple-element.15.refs_0_, bf16[32,16,128]{2,1,0:T(8,128)(2,1)S(1)} %get-tuple-element.16.refs_1_, ...), custom_call_target="tpu_custom_call" | custom-call | tf_op jit(solution)/shard_map/write_out/pallas_call | solution.py:539

commit v6 on v5

--- a/solution.py
+++ b/solution.py
@@ -80,6 +80,14 @@
         x,
         jnp.where(layer > 0, roll(x, 1), zero(x)),
     ]
+
+
+def merge_layers(z):
+    outs = z.shape[0] // 3
+    layer = lane_of((outs, 128)) % 32
+    low = jnp.where(layer > 0, roll(z[:outs], 1), 0.0)
+    high = jnp.where(layer < 31, roll(z[2 * outs :], -1), 0.0)
+    return z[outs : 2 * outs] + low + high
 
 
 def conv_rows(src, count, weight, outs, sink):
@@ -236,13 +244,16 @@
         dst[1:17, 32:64, :] = rows
         dst[1:17, 64:96, :] = jnp.where(lane >= 96, zero(rows), roll(rows, -32))
 
-    def fine_windows_rim(dst, arrived):
-        cols, rim = halo_parts(arrived)
+    def fine_windows_cols(dst, arrived):
+        cols, _ = halo_parts(arrived)
         lane = lane_of((16, 32, 128))
         left = jnp.concatenate(unpack_column(cols[0], 0), axis=0)
         right = jnp.concatenate(unpack_column(cols[1], 96), axis=0)
         dst[1:17, 0:32, :] = jnp.where(lane < lo32, left, dst[1:17, 0:32, :])
         dst[1:17, 64:96, :] = jnp.where(lane >= hi96, right, dst[1:17, 64:96, :])
+
+    def fine_windows_rows(dst, arrived):
+        _, rim = halo_parts(arrived)
         lane = lane_of((1, 32, 128))
         for k, at in ((0, 0), (3, 17)):
             rows, left, right = rim[k], roll(rim[k + 1], 32), roll(rim[k + 2], 96)
@@ -254,7 +265,15 @@
                 lane >= hi96, right, jnp.where(lane >= 96, zero(rows), roll(rows, -32))
             )
 
+    w_left, w_right = [
+        side_by_side([wa_f[:, 96 * a + 32 * b : 96 * a + 32 * b + 32] for a in range(3)])
+        for b in (0, 2)
+    ]
+    w_above, w_below = wa_f[:, 0:96], wa_f[:, 192:288]
+    sfa[0] = jnp.zeros((96, 128), BF)
+    sfa[17] = jnp.zeros((96, 128), BF)
     fine_windows_own(sfa, x)
+    conv_rows(sfa, 16, wa_f, 32, lin_a_s)
 
     halo_x.wait_send()
     departures.remove(halo_x)
@@ -262,8 +281,25 @@
         1, (colf_s.at[0], colf_s.at[1]), (fold_s.at[7], fold_s.at[0]), rf
     )
     halo_x.wait_recv()
-    fine_windows_rim(sfa, rx)
-    conv_rows(sfa, 16, wa_f, 32, lin_a_s)
+
+    def side(packed, weight):
+        lane = lane_of((1, 32, 128))
+        before = jnp.where(lane >= 32, roll(packed[3:4], 32), zero(packed))
+        after = jnp.where(lane < 96, roll(packed[0:1], -32), zero(packed))
+        rows = jnp.concatenate([before, packed, after], axis=0)
+        z = dot(weight, side_by_side([rows[q : q + 3].reshape(96, 128) for q in range(4)]))
+        return jnp.concatenate(
+            [merge_layers(z[:, 128 * q : 128 * q + 128])[None] for q in range(4)], axis=0
+        )
+
+    cols, _ = halo_parts(rx)
+    left = jnp.concatenate(unpack_column(side(cols[0], w_left), 0), axis=0)
+    right = jnp.concatenate(unpack_column(side(cols[1], w_right), 96), axis=0)
+    lane = lane_of((16, 32, 128))
+    lin_a_s[...] += jnp.where(lane < lo32, left, jnp.where(lane >= hi96, right, 0.0))
+    fine_windows_rows(sfa, rx)
+    lin_a_s[0] += merge_layers(dot(w_above, sfa[0]))
+    lin_a_s[15] += merge_layers(dot(w_below, sfa[17]))
     lin_a = lin_a_s[...]
     hidden = (lin_a / (1.0 + jnp.exp(-lin_a))).astype(BF).astype(F32).reshape(8, 2, 32, 128)
     coarse = (0.25 * pool_columns(hidden[:, 0] + hidden[:, 1])).astype(BF)
@@ -302,6 +338,7 @@
     scb[own_rows, 32:64, :] = coarse
     scb[own_rows, 64:96, :] = jnp.where(lane < 64, roll(coarse, -32), zero(coarse))
 
+    fine_windows_cols(sfa, rx)
     for r in range(16):
         sft[r] = sfa[r : r + 3].reshape(288, 128).T
 
@@ -445,7 +482,8 @@
 
     fine_windows_own(sga, grad_a)
     halo_g.wait_recv()
-    fine_windows_rim(sga, rg)
+    fine_windows_cols(sga, rg)
+    fine_windows_rows(sga, rg)
     conv_rows(sga, 16, wa_b, 32, gi_s)
     gi_ref[...] = jnp.transpose(gi_s[...].astype(BF), (1, 0, 2))
 

time: 40.3 us -> 40.2 us (level)
  no operation moved by 1% of the time
where the time goes in v6:
time: 40.2 us; the launch traced here: 40.1 us
  Pallas kernels  39.5 us (98%)
  between operations  0.64 us (2%)
    pallas_call x1, Pallas kernels, shards(): pl.pallas_call(functools.partial(kernel, n_phi, n_eta, 1.0 / math.sqrt(ce...  38.4 us
    pallas_call x1, Pallas kernels, shards(): pl.pallas_call(writer, out_shape=tuple((jax.ShapeDtypeStruct(s, t) for s,...  1.04 us

profile of v6, /device:TPU:1, one launch (start us, length us, event | category | flops | bytes accessed | tf_op | source)
XLA Modules:
  0.0 40.1 jit_solution(18386319135631844104)
XLA Ops:
  0.6 38.4 %block_step.1 = (bf16[32,16,128]{2,1,0:T(8,128)(2,1)S(1)}, bf16[32,16,128]{2,1,0:T(8,128)(2,1)S(1)}, f32[27,32,32]{2,1,0:T(8,128)S(1)}, f32[27,32,64]{2,1,0:T(8,128)S(1)}, f32[32,64]{1,0:T(8,128)S(1)}) custom-call(bf16[32,16,128]{2,1,0:T(8,128)(2,1)} %refs_0_.1, bf16[32,16,128]{2,1,0:T(8,128)(2,1)} %refs_1_.1, bf16[27,32,32]{2,1,0:T(8,128)(2,1)} %refs_2_.1, ...), custom_call_target="tpu_custom_call" | custom-call | tf_op jit(solution)/shard_map/block_step/pallas_call | solution.py:568
  39.1 1.0 %write_out.1 = (bf16[32,16,128]{2,1,0:T(8,128)(2,1)}, bf16[32,16,128]{2,1,0:T(8,128)(2,1)}, f32[27,32,32]{2,1,0:T(8,128)}, f32[27,32,64]{2,1,0:T(8,128)}, f32[32,64]{1,0:T(8,128)}) custom-call(bf16[32,16,128]{2,1,0:T(8,128)(2,1)S(1)} %get-tuple-element.15.refs_0_, bf16[32,16,128]{2,1,0:T(8,128)(2,1)S(1)} %get-tuple-element.16.refs_1_, ...), custom_call_target="tpu_custom_call" | custom-call | tf_op jit(solution)/shard_map/write_out/pallas_call | solution.py:577

commit v7 on v6

--- a/solution.py
+++ b/solution.py
@@ -272,6 +272,9 @@
     w_above, w_below = wa_f[:, 0:96], wa_f[:, 192:288]
     sfa[0] = jnp.zeros((96, 128), BF)
     sfa[17] = jnp.zeros((96, 128), BF)
+    for t in range(28, PLANE):
+        pa[t] = jnp.zeros((8, 128), BF)
+        pb[t] = jnp.zeros((16, 128), BF)
     fine_windows_own(sfa, x)
     conv_rows(sfa, 16, wa_f, 32, lin_a_s)
 
@@ -398,8 +401,6 @@
     for i in range(9):
         pb[18 + i] = rest[16 * i : 16 * i + 16].astype(BF)
     pb[27] = side_by_side([sum_m[0:16], sum_m[16:32]]).astype(BF)
-    for t in range(28, PLANE):
-        pb[t] = jnp.zeros((16, 128), BF)
 
     def spread(buf, dst, k):
         for i, step in enumerate(steps):
@@ -428,21 +429,9 @@
     rest = jnp.concatenate([rest, jnp.zeros((32, 32), F32)], axis=1)
     for i in range(4):
         pa[24 + i] = rest[8 * i : 8 * i + 8].astype(BF)
-    for t in range(28, PLANE):
-        pa[t] = jnp.zeros((8, 128), BF)
     spread_a = spread(pa, ra, 1)
     colg_s[0] = pack_column(grad_a, 4, 96)
     colg_s[1] = pack_column(grad_a, 4, 0)
-    projected = dot(mix, side_by_side([gated[r] for r in range(4)])).astype(BF).astype(F32)
-    projected = jnp.concatenate(
-        [projected[:, 128 * r : 128 * (r + 1)][None] for r in range(4)], axis=0
-    )
-    projected = widen_pairs(projected)
-    output = jnp.concatenate(
-        [(hidden[:, i] + projected)[:, None] for i in range(2)], axis=1
-    ).reshape(16, 32, 128)
-    out_ref[...] = jnp.transpose(output.astype(BF), (1, 0, 2))
-
     def cross(copy, buf, arrived, mine, slots, k):
         copy.wait_recv()
         total = buf[me1].astype(F32)
@@ -476,6 +465,16 @@
     halo_g = halo_start(
         3, (colg_s.at[0], colg_s.at[1]), (g_s.at[15], g_s.at[0]), rg
     )
+
+    projected = dot(mix, side_by_side([gated[r] for r in range(4)])).astype(BF).astype(F32)
+    projected = jnp.concatenate(
+        [projected[:, 128 * r : 128 * (r + 1)][None] for r in range(4)], axis=0
+    )
+    projected = widen_pairs(projected)
+    output = jnp.concatenate(
+        [(hidden[:, i] + projected)[:, None] for i in range(2)], axis=1
+    ).reshape(16, 32, 128)
+    out_ref[...] = jnp.transpose(output.astype(BF), (1, 0, 2))
 
     gather_b = gather(cross_b, rb2, xb3, resb, 4)
     gather_a = gather(cross_a, ra2, xa3, resa, 5)

time: 40.2 us -> 40.2 us (level)
  no operation moved by 1% of the time
where the time goes in v7:
time: 40.2 us; the launch traced here: 40.1 us
  Pallas kernels  39.5 us (98%)
  between operations  0.64 us (2%)
    pallas_call x1, Pallas kernels, shards(): pl.pallas_call(functools.partial(kernel, n_phi, n_eta, 1.0 / math.sqrt(ce...  38.4 us
    pallas_call x1, Pallas kernels, shards(): pl.pallas_call(writer, out_shape=tuple((jax.ShapeDtypeStruct(s, t) for s,...  1.04 us

profile of v7, /device:TPU:1, one launch (start us, length us, event | category | flops | bytes accessed | tf_op | source)
XLA Modules:
  0.0 40.1 jit_solution(4540731657629095695)
XLA Ops:
  0.6 38.4 %block_step.1 = (bf16[32,16,128]{2,1,0:T(8,128)(2,1)S(1)}, bf16[32,16,128]{2,1,0:T(8,128)(2,1)S(1)}, f32[27,32,32]{2,1,0:T(8,128)S(1)}, f32[27,32,64]{2,1,0:T(8,128)S(1)}, f32[32,64]{1,0:T(8,128)S(1)}) custom-call(bf16[32,16,128]{2,1,0:T(8,128)(2,1)} %refs_0_.1, bf16[32,16,128]{2,1,0:T(8,128)(2,1)} %refs_1_.1, bf16[27,32,32]{2,1,0:T(8,128)(2,1)} %refs_2_.1, ...), custom_call_target="tpu_custom_call" | custom-call | tf_op jit(solution)/shard_map/block_step/pallas_call | solution.py:567
  39.1 1.0 %write_out.1 = (bf16[32,16,128]{2,1,0:T(8,128)(2,1)}, bf16[32,16,128]{2,1,0:T(8,128)(2,1)}, f32[27,32,32]{2,1,0:T(8,128)}, f32[27,32,64]{2,1,0:T(8,128)}, f32[32,64]{1,0:T(8,128)}) custom-call(bf16[32,16,128]{2,1,0:T(8,128)(2,1)S(1)} %get-tuple-element.15.refs_0_, bf16[32,16,128]{2,1,0:T(8,128)(2,1)S(1)} %get-tuple-element.16.refs_1_, ...), custom_call_target="tpu_custom_call" | custom-call | tf_op jit(solution)/shard_map/write_out/pallas_call | solution.py:576
